TPU v7x, 256 devices: a whole 4x4x8 slice. The times are simulated.
256 devices in a mesh: row: 16 (over y, z_hi), col: 16 (over x, z_lo, core).
Axes of the slice: x: 4, y: 4, z: 8 (z_hi: 4, z_lo: 2; z = z_hi * 2 + z_lo), core: 2. Of those that a mesh axis runs over, the one named last changes fastest.
Arguments:
- pair_rep: bfloat16 [2048, 2048, 128], P('row', 'col'), may hold values from -8 to 8
- row_ids: int32 [32], P('row'), may hold values from 0 to 2047, as said below
- pad_mask: int32 [2048], P('col'), may hold values from 0 to 1, as said below
- ln_gain: float32 [128], replicated, may hold values from 0.25 to 1.75
- ln_bias: float32 [128], replicated, may hold values from -2 to 2
- w_query: bfloat16 [128, 128], replicated, may hold values from -2 to 2
- w_key: bfloat16 [128, 128], replicated, may hold values from -2 to 2
- w_value: bfloat16 [128, 128], replicated, may hold values from -0.5 to 0.5
- w_gate: bfloat16 [128, 128], replicated, may hold values from -0.5 to 0.5
- gate_bias: float32 [128], replicated, may hold values from -4 to 4
- w_bias: bfloat16 [128, 4], replicated, may hold values from -0.5 to 0.5
- w_out: bfloat16 [128, 128], replicated, may hold values from -0.5 to 0.5
Outputs:
- update: bfloat16 [32, 2048, 128], P('col', 'row')
Inputs may be any that keep to these rules, and one draw needn't show every extreme that they name: `row_ids`: entries t * 2 to t * 2 + 1 are distinct and lie in [t * 128, (t + 1) * 128). `pad_mask`: A prefix of the tokens is real and the rest is padding; the first 513 tokens are real.
All inputs are finite; a program needn't handle non-finite values.
Results may differ from a plain program's by a relative error of at most 0.023.
Values may be sent and summed in bfloat16 or wider, within the bound.
No kernel may reach another device: no remote copies, remote signals or barrier semaphores. Data moves between devices by JAX's collectives and lax.ppermute only.
A program may use at most 128 MiB of HBM per device.

v0:
```python
import jax
import jax.numpy as jnp
from jax import lax
from jax.experimental import pallas as pl
from jax.experimental.pallas import tpu as pltpu
from jax.sharding import PartitionSpec as P


MASKED = -1e30
STATS = 16
BIAS_ROWS = 16
AXES = ("row", "col")
F32 = jnp.float32
BF16 = jnp.bfloat16
VMEM = pltpu.VMEM


def params(mib=16):
    return pltpu.CompilerParams(vmem_limit_bytes=mib << 20)


def cost(flops, moved, exps=0):
    return pl.CostEstimate(flops=flops, bytes_accessed=moved, transcendentals=exps)


def whole():
    return pl.BlockSpec(memory_space=VMEM)


def layer_norm(values, ln_gain, ln_bias):
    values = values.astype(F32)
    values = values - jnp.mean(values, axis=-1, keepdims=True)
    spread = jnp.mean(values * values, axis=-1, keepdims=True)
    return (values * lax.rsqrt(spread + 1e-05) * ln_gain + ln_bias).astype(BF16)


def fetch_kernel(row_ids, pair_rep, ln_gain, ln_bias, out, ids, rows, gain, shift, sems):
    copies = [
        pltpu.make_async_copy(row_ids, ids, sems.at[0]),
        pltpu.make_async_copy(ln_gain, gain, sems.at[1]),
        pltpu.make_async_copy(ln_bias, shift, sems.at[2]),
    ]
    for copy in copies:
        copy.start()
    copies[0].wait()
    for t in range(rows.shape[0]):
        at = lax.rem(ids[t], pair_rep.shape[0])
        copies.append(pltpu.make_async_copy(pair_rep.at[at], rows.at[t], sems.at[3 + t]))
        copies[-1].start()
    copies[1].wait()
    copies[2].wait()
    for t in range(rows.shape[0]):
        copies[3 + t].wait()
        out[t] = layer_norm(rows[t], gain[...], shift[...])


def fetch(row_ids, pair_rep, ln_gain, ln_bias):
    _, tokens, width = pair_rep.shape
    count = row_ids.shape[0]
    return pl.pallas_call(
        fetch_kernel,
        in_specs=[pl.BlockSpec(memory_space=pltpu.HBM)] * 4,
        out_specs=whole(),
        out_shape=jax.ShapeDtypeStruct((count, tokens, width), BF16),
        scratch_shapes=[
            pltpu.SMEM((count,), jnp.int32),
            VMEM((count, tokens, width), BF16),
            VMEM((1, width), F32),
            VMEM((1, width), F32),
            pltpu.SemaphoreType.DMA((3 + count,)),
        ],
        compiler_params=params(60),
        cost_estimate=cost(10 * count * tokens * width, 4 * count * tokens * width),
        name="fetch",
    )(row_ids, pair_rep, ln_gain, ln_bias)


def bias_kernel(
    pair_rep, ln_gain, ln_bias, w_bias, pad_mask, out, rows, lifted, gain, shift, weights, live, sems
):
    heads, block, tokens = out.shape
    width = rows.shape[2]
    small = [(ln_gain, gain), (ln_bias, shift), (w_bias, weights), (pad_mask, live)]
    copies = [pltpu.make_async_copy(a, b, sems.at[i]) for i, (a, b) in enumerate(small)]
    for i in range(0, block, BIAS_ROWS):
        part = pl.ds(i, BIAS_ROWS)
        at = len(small) + i // BIAS_ROWS
        copies.append(pltpu.make_async_copy(pair_rep.at[part], rows.at[part], sems.at[at]))
    for copy in copies:
        copy.start()
    for copy in copies[: len(small)]:
        copy.wait()
    plain = weights[...].astype(F32)
    scaled = plain * gain[...]
    high = scaled.astype(BF16).astype(F32)
    at = lax.broadcasted_iota(jnp.int32, (heads * 8, width), 0) % 8
    offset = jnp.sum(plain * shift[...], axis=1, keepdims=True)
    offset = jnp.broadcast_to(offset[:, None], (heads, 8, tokens))
    for part, value in enumerate((high, scaled - high)):
        value = jnp.broadcast_to(value[:, None], (heads, 8, width)).reshape(heads * 8, width)
        for j in range(8):
            placed = jnp.where(at == j, value, 0.0).astype(BF16)
            lifted[j, part * heads * 8 : (part + 1) * heads * 8] = placed
    real = live[...] > 0
    sub = lax.broadcasted_iota(jnp.int32, (8, tokens), 0)

    def eight(group, carry):
        total = jnp.zeros((2 * heads * 8, tokens), F32)
        spread = jnp.zeros((8, tokens), F32)
        for j in range(8):
            values = rows[group * 8 + j].T.astype(F32)
            values = values - jnp.sum(values, axis=0, keepdims=True) * (1.0 / width)
            total += jnp.dot(lifted[j], values.astype(BF16), preferred_element_type=F32)
            squares = jnp.sum(values * values, axis=0, keepdims=True)
            spread = jnp.where(sub == j, squares, spread)
        scale = lax.rsqrt(spread * (1.0 / width) + 1e-05)
        total = total[: heads * 8] + total[heads * 8 :]
        total = total.reshape(heads, 8, tokens) * scale[None] + offset
        out[:, pl.ds(pl.multiple_of(group * 8, 8), 8), :] = jnp.where(real, total, MASKED)
        return carry

    for i in range(0, block, BIAS_ROWS):
        copies[len(small) + i // BIAS_ROWS].wait()
        lax.fori_loop(i // 8, (i + BIAS_ROWS) // 8, eight, 0)


def pair_bias(pair_rep, ln_gain, ln_bias, w_bias, pad_mask):
    block, tokens, width = pair_rep.shape
    heads = w_bias.shape[1]
    return pl.pallas_call(
        bias_kernel,
        in_specs=[pl.BlockSpec(memory_space=pltpu.HBM)] * 5,
        out_specs=whole(),
        out_shape=jax.ShapeDtypeStruct((heads, block, tokens), F32),
        scratch_shapes=[
            VMEM((block, tokens, width), BF16),
            VMEM((8, 2 * heads * 8, width), BF16),
            VMEM((1, width), F32),
            VMEM((1, width), F32),
            VMEM((heads, width), BF16),
            VMEM((1, tokens), jnp.int32),
            pltpu.SemaphoreType.DMA((4 + block // BIAS_ROWS,)),
        ],
        compiler_params=params(60),
        cost_estimate=cost(4 * block * tokens * width, 2 * block * tokens * width),
        name="pair_bias",
    )(pair_rep, ln_gain, ln_bias, w_bias.T, pad_mask.reshape(1, tokens))


def project_kernel(*refs):
    blocks, (w_key, w_value, keys, values) = refs[:-4], refs[-4:]
    block, width = blocks[0].shape[-2:]
    row, col = lax.axis_index("row"), lax.axis_index("col")
    y, h, x, q = row // 4, row % 4, col // 4, col % 4
    places = [(x - y + s + 4) % 4 for s in range(4)]
    flips = [((h - i + 4) % 4) ^ q for i in range(4)]
    places += [(f // 2) + (f % 2) * 2 for f in flips]
    weights = jnp.concatenate([w_key[...], w_value[...]], axis=1)
    for s in range(4):
        for i in range(4):
            for t in range(2):
                both = jnp.dot(blocks[s][i, t], weights, preferred_element_type=F32)
                both = both.astype(BF16)
                at = pl.ds(pl.multiple_of(places[4 + i] * block, block), block)
                keys[places[s], t, :, at] = both[:, :width].T
                values[places[s], t, at, :] = both[:, width:]


def project(blocks, w_key, w_value):
    block, width = blocks[0].shape[-2:]
    return pl.pallas_call(
        project_kernel,
        in_specs=[whole()] * (len(blocks) + 2),
        out_specs=[whole(), whole()],
        out_shape=[
            jax.ShapeDtypeStruct((4, 2, width, 4 * block), BF16),
            jax.ShapeDtypeStruct((4, 2, 4 * block, width), BF16),
        ],
        compiler_params=params(),
        cost_estimate=cost(2 * 4096 * 128 * 256, 3 << 20),
        name="project",
    )(*blocks, w_key, w_value)


def attend_kernel(rows, keys, values, bias_a, bias_b, bias_c, bias_d, w_query, out):
    block, width = rows.shape[1:]
    heads = bias_a.shape[0]
    head_dim = width // heads
    lane = lax.broadcasted_iota(jnp.int32, (block, width), 1)
    for t in range(2):
        query = jnp.dot(rows[t], w_query[...], preferred_element_type=F32)
        query = (query * (head_dim**-0.5)).astype(BF16)
        key = keys[0, t]
        value = jnp.concatenate([values[0, t], jnp.ones((4 * block, width), BF16)], axis=1)
        summed = jnp.zeros((block, width), F32)
        stats = jnp.zeros((block, width), F32)
        for h in range(heads):
            mine = lane // head_dim == h
            part = jnp.where(mine, query, jnp.zeros_like(query))
            scores = jnp.dot(part, key, preferred_element_type=F32)
            bias = [bias_a[h], bias_b[h], bias_c[h], bias_d[h]]
            scores = scores + jnp.concatenate(bias, axis=1)
            peak = jnp.max(scores, axis=1, keepdims=True)
            expo = jnp.exp(scores - peak).astype(BF16)
            result = jnp.dot(expo, value, preferred_element_type=F32)
            summed = jnp.where(mine, result[:, :width], summed)
            total = result[:, width:]
            high = peak.astype(BF16).astype(F32)
            middle = (peak - high).astype(BF16).astype(F32)
            for i, column in enumerate((high, middle, peak - high - middle, total)):
                stats = jnp.where(lane == i * heads + h, column, stats)
        out[t, :block] = summed.astype(BF16)
        out[t, block:] = stats.T[:STATS].astype(BF16)


def attend(s, rows, keys, values, biases, w_query):
    _, block, width = rows.shape
    parts = [pl.BlockSpec((1, *v.shape[1:]), lambda i: (s, 0, 0, 0)) for v in (keys, values)]
    full = [
        pl.BlockSpec(v.shape, lambda i, n=v.ndim: (0,) * n) for v in (rows, *biases, w_query)
    ]
    return pl.pallas_call(
        attend_kernel,
        grid=(1,),
        in_specs=[full[0], *parts, *full[1:]],
        out_specs=pl.BlockSpec((2, block + STATS, width), lambda i: (0, 0, 0)),
        out_shape=jax.ShapeDtypeStruct((2, block + STATS, width), BF16),
        compiler_params=params(),
        cost_estimate=cost(8 * 2 * 128 * 512 * 128 * 2, 2 << 20, 2 * 4 * 128 * 512),
    )(rows, keys, values, *biases, w_query)


def finish_kernel(first, second, third, fourth, rows, w_gate, gate_bias, w_out, out):
    block, width = rows.shape[1:]
    heads = STATS // 4
    head_dim = width // heads
    parts = (first, second, third, fourth)
    source = lax.broadcasted_iota(jnp.int32, (width, 4 * width), 0)
    target = lax.broadcasted_iota(jnp.int32, (width, 4 * width), 1) // head_dim
    meets = (source % STATS == target) & (source < 2 * STATS)
    spreading = jnp.where(meets, 1.0, 0.0).astype(BF16)
    for t in range(2):
        peaks, totals = [], []
        for part in parts:
            stats = part[t, block:].astype(F32)
            peaks.append(stats[:heads] + stats[heads : 2 * heads] + stats[2 * heads : 3 * heads])
            totals.append(stats[3 * heads :])
        overall = jnp.maximum(jnp.maximum(peaks[0], peaks[1]), jnp.maximum(peaks[2], peaks[3]))
        factors = [jnp.exp(peak - overall) for peak in peaks]
        whole_total = sum(f * total for f, total in zip(factors, totals))
        factors = jnp.concatenate([f / whole_total for f in factors], axis=0)
        high = factors.astype(BF16)
        low = (factors - high.astype(F32)).astype(BF16)
        padding = jnp.zeros((width - 2 * STATS, block), BF16)
        factors = jnp.concatenate([high, low, padding], axis=0).T
        wide = jnp.dot(factors, spreading, preferred_element_type=F32)
        attended = jnp.zeros((block, width), F32)
        for p, part in enumerate(parts):
            attended += wide[:, p * width : (p + 1) * width] * part[t, :block].astype(F32)
        gate = jnp.dot(rows[t], w_gate[...], preferred_element_type=F32) + gate_bias[...]
        gate = jax.nn.sigmoid(gate).astype(BF16).astype(F32)
        gated = (gate * attended).astype(BF16)
        out[t] = jnp.dot(gated, w_out[...], preferred_element_type=F32).astype(BF16)


def finish(parts, rows, w_gate, gate_bias, w_out):
    return pl.pallas_call(
        finish_kernel,
        in_specs=[whole()] * 8,
        out_specs=whole(),
        out_shape=jax.ShapeDtypeStruct(rows.shape, BF16),
        compiler_params=params(),
        cost_estimate=cost(4 * 256 * 128 * 128, 1 << 19),
        name="finish",
    )(*parts, rows, w_gate, gate_bias, w_out)


def moves(target):
    pairs = []
    for i in range(256):
        y, h, x, q = i // 64, i // 16 % 4, i // 4 % 4, i % 4
        a, b, c, d = target(y, h, x, q)
        pairs.append((i, ((a % 4 * 4 + b % 4) * 4 + c % 4) * 4 + d % 4))
    return pairs


def send(value, target):
    return lax.ppermute(value, AXES, moves(target))


def body(
    pair_rep,
    row_ids,
    pad_mask,
    ln_gain,
    ln_bias,
    w_query,
    w_key,
    w_value,
    w_gate,
    gate_bias,
    w_bias,
    w_out,
):
    _, _, width = pair_rep.shape
    ln_gain, ln_bias = ln_gain.reshape(1, width), ln_bias.reshape(1, width)
    piece = fetch(row_ids, pair_rep, ln_gain, ln_bias)
    low = []
    for i in range(4):
        low.append(send(piece, lambda y, h, x, q, i=i: (y, q + i, x, h)))

    bias = pair_bias(pair_rep, ln_gain, ln_bias, w_bias, pad_mask)
    bias_z = send(bias, lambda y, h, x, q: (y, h, x, q ^ 2))
    bias_c = send(bias, lambda y, h, x, q: (y, h, x, q ^ 1))
    bias_zc = send(bias_z, lambda y, h, x, q: (y, h, x, q ^ 1))
    biases = (bias, bias_z, bias_c, bias_zc)

    own = jnp.stack(low)
    rows_kv = [own]
    for s in (1, 2, 3):
        rows_kv.append(send(own, lambda y, h, x, q, s=s: (y + s, h, x, q)))
    rows_q = []
    for s in range(4):
        rows_q.append(send(low[0], lambda y, h, x, q, s=s: (x, h, y + s, q)))

    keys, values = project(rows_kv, w_key, w_value)
    parts = []
    for s in (2, 1, 3, 0):
        part = attend(s, rows_q[s], keys, values, biases, w_query)
        if s:
            part = send(part, lambda y, h, x, q, s=s: (y, h, x - s, q))
        parts.append(part)
    return finish(parts, rows_q[0], w_gate, gate_bias.reshape(1, width), w_out)


def solution(mesh):
    return jax.shard_map(
        body,
        mesh=mesh,
        in_specs=(P("row", "col", None), P("row"), P("col")) + (P(),) * 9,
        out_specs=P("col", "row", None),
        check_vma=False,
    )
```

profile of v0, /device:TPU:24, one launch (start us, length us, event | category | flops | bytes accessed | tf_op | source)
XLA Modules:
  0.0 68.5 jit_solution(1576105755645239392)
XLA Ops:
  0.0 7.4 %pair_bias.1.bias_a = f32[4,128,128]{2,1,0:T(8,128)} custom-call(bf16[128,128,128]{2,1,0:T(8,128)(2,1)} %pair_rep.3, f32[1,128]{1,0:T(1,128)} %bitcast.14, f32[1,128]{1,0:T(1,128)} %bitcast.16, bf16[4,128]{1,0:T(4,128)(2,1)} %bitcast.18, s32[1,128]{1,0:T(1,128)} %bitcast.19), custom_call_target="tpu_custom_call" | custom-call | flops 8388608 | bytes 4194304 | tf_op jit(solution)/shard_map/pair_bias/pallas_call | solution.py:130
  7.4 2.0 %collective-permute-start.8 = (f32[4,128,128]{2,1,0:T(8,128)}, f32[4,128,128]{2,1,0:T(8,128)S(1)}, u32[]{:S(2)}, u32[]{:S(2)}) collective-permute-start(f32[4,128,128]{2,1,0:T(8,128)} %pair_bias.1.bias_a), channel_id=1, source_target_pairs={{0,2},{1,3},{2,0},{3,1},{4,6},{5,7},{6,4},{7,5},{8,10},{9,11},{10,... | collective-permute-start | bytes 786440 | tf_op jit(solution)/shard_map/ppermute | solution.py:288
  9.4 2.5 %fetch.1 = bf16[2,128,128]{2,1,0:T(8,128)(2,1)} custom-call(s32[2]{0:T(128)} %row_ids.1, bf16[128,128,128]{2,1,0:T(8,128)(2,1)} %pair_rep.3, f32[1,128]{1,0:T(1,128)} %bitcast.15, f32[1,128]{1,0:T(1,128)} %bitcast.17), custom_call_target="tpu_custom_call" | custom-call | flops 327680 | bytes 131072 | tf_op jit(solution)/shard_map/fetch/pallas_call | solution.py:60
  11.9 1.5 %collective-permute-start = (bf16[2,128,128]{2,1,0:T(8,128)(2,1)}, bf16[2,128,128]{2,1,0:T(8,128)(2,1)S(1)}, u32[]{:S(2)}, u32[]{:S(2)}) collective-permute-start(bf16[2,128,128]{2,1,0:T(8,128)(2,1)} %fetch.1), channel_id=1, source_target_pairs={{0,0},{1,16},{2,32},{3,48},{4,4},{5,20},{6,36},{7,52},{8,8},{9,24}... | collective-permute-start | bytes 196616 | tf_op jit(solution)/shard_map/ppermute | solution.py:288
  13.4 5.9 %collective-permute-start.4 = (bf16[2,128,128]{2,1,0:T(8,128)(2,1)}, bf16[2,128,128]{2,1,0:T(8,128)(2,1)S(1)}, u32[]{:S(2)}, u32[]{:S(2)}) collective-permute-start(bf16[2,128,128]{2,1,0:T(8,128)(2,1)} %fetch.1), channel_id=1, source_target_pairs={{0,48},{1,0},{2,16},{3,32},{4,52},{5,4},{6,20},{7,36},{8,56},{9,8}... | collective-permute-start | bytes 196616 | tf_op jit(solution)/shard_map/ppermute | solution.py:288
  19.3 3.4 %collective-permute-start.3 = (bf16[2,128,128]{2,1,0:T(8,128)(2,1)}, bf16[2,128,128]{2,1,0:T(8,128)(2,1)S(1)}, u32[]{:S(2)}, u32[]{:S(2)}) collective-permute-start(bf16[2,128,128]{2,1,0:T(8,128)(2,1)} %fetch.1), channel_id=1, source_target_pairs={{0,32},{1,48},{2,0},{3,16},{4,36},{5,52},{6,4},{7,20},{8,40},{9,56... | collective-permute-start | bytes 196616 | tf_op jit(solution)/shard_map/ppermute | solution.py:288
  22.7 2.8 %collective-permute-start.2 = (bf16[2,128,128]{2,1,0:T(8,128)(2,1)}, bf16[2,128,128]{2,1,0:T(8,128)(2,1)S(1)}, u32[]{:S(2)}, u32[]{:S(2)}) collective-permute-start(bf16[2,128,128]{2,1,0:T(8,128)(2,1)} %fetch.1), channel_id=1, source_target_pairs={{0,16},{1,32},{2,48},{3,0},{4,20},{5,36},{6,52},{7,4},{8,24},{9,40... | collective-permute-start | bytes 196616 | tf_op jit(solution)/shard_map/ppermute | solution.py:288
  25.5 0.0 collective-permute-done.4
  25.5 2.0 %collective-permute-done.3 = bf16[2,128,128]{2,1,0:T(8,128)(2,1)S(1)} collective-permute-done((bf16[2,128,128]{2,1,0:T(8,128)(2,1)}, bf16[2,128,128]{2,1,0:T(8,128)(2,1)S(1)}, u32[]{:S(2)}, u32[]{:S(2)}) %collective-permute-start.3) | collective-permute-done | bytes 65568 | tf_op jit(solution)/shard_map/ppermute | solution.py:288
  27.5 0.8 %collective-permute-done.2 = bf16[2,128,128]{2,1,0:T(8,128)(2,1)S(1)} collective-permute-done((bf16[2,128,128]{2,1,0:T(8,128)(2,1)}, bf16[2,128,128]{2,1,0:T(8,128)(2,1)S(1)}, u32[]{:S(2)}, u32[]{:S(2)}) %collective-permute-start.2) | collective-permute-done | bytes 65568 | tf_op jit(solution)/shard_map/ppermute | solution.py:288
  28.3 0.3 collective-permute-start.5
  28.6 2.6 %collective-permute-start.6 = (bf16[4,2,128,128]{3,2,1,0:T(8,128)(2,1)S(1)}, bf16[4,2,128,128]{3,2,1,0:T(8,128)(2,1)S(1)}, u32[]{:S(2)}, u32[]{:S(2)}) collective-permute-start(bf16[4,2,128,128]{3,2,1,0:T(8,128)(2,1)S(1)} %pad_maximum_fusion.refs_0_), channel_id=1, source_target_pairs={{0,128},{1,129},{2,130},{3,131},{4,132},{5,133},{6,134},{7,135},{8... | collective-permute-start | bytes 786440 | tf_op jit(solution)/shard_map/ppermute | solution.py:288
  31.2 0.0 collective-permute-start.7
  31.2 0.0 collective-permute-start.9
  31.2 0.0 collective-permute-done.8.bias_b
  31.2 0.5 collective-permute-start.10
  31.7 5.8 %collective-permute-done.5.refs_1_ = bf16[4,2,128,128]{3,2,1,0:T(8,128)(2,1)S(1)} collective-permute-done((bf16[4,2,128,128]{3,2,1,0:T(8,128)(2,1)S(1)}, bf16[4,2,128,128]{3,2,1,0:T(8,128)(2,1)S(1)}, u32[]{:S(2)}, u32[]{:S(2)}) %collective-permute-start.5) | collective-permute-done | bytes 262176 | tf_op jit(solution)/shard_map/ppermute | solution.py:288
  37.6 1.2 %collective-permute-start.1 = (bf16[2,128,128]{2,1,0:T(8,128)(2,1)S(1)}, bf16[2,128,128]{2,1,0:T(8,128)(2,1)S(1)}, u32[]{:S(2)}, u32[]{:S(2)}) collective-permute-start(bf16[2,128,128]{2,1,0:T(8,128)(2,1)S(1)} %collective-permute-done), channel_id=1, source_target_pairs={{0,8},{1,9},{2,10},{3,11},{4,72},{5,73},{6,74},{7,75},{8,136},{9,1... | collective-permute-start | bytes 196616 | tf_op jit(solution)/shard_map/ppermute | solution.py:288
  38.8 0.5 collective-permute-done.6.refs_2_
  39.4 6.4 %collective-permute-start.12 = (bf16[2,128,128]{2,1,0:T(8,128)(2,1)S(1)}, bf16[2,128,128]{2,1,0:T(8,128)(2,1)S(1)}, u32[]{:S(2)}, u32[]{:S(2)}) collective-permute-start(bf16[2,128,128]{2,1,0:T(8,128)(2,1)S(1)} %collective-permute-done), channel_id=1, source_target_pairs={{0,4},{1,5},{2,6},{3,7},{4,68},{5,69},{6,70},{7,71},{8,132},{9,133... | collective-permute-start | bytes 196616 | tf_op jit(solution)/shard_map/ppermute | solution.py:288
  45.8 1.8 %collective-permute-start.14 = (bf16[2,128,128]{2,1,0:T(8,128)(2,1)S(1)}, bf16[2,128,128]{2,1,0:T(8,128)(2,1)S(1)}, u32[]{:S(2)}, u32[]{:S(2)}) collective-permute-start(bf16[2,128,128]{2,1,0:T(8,128)(2,1)S(1)} %collective-permute-done), channel_id=1, source_target_pairs={{0,12},{1,13},{2,14},{3,15},{4,76},{5,77},{6,78},{7,79},{8,140},{9... | collective-permute-start | bytes 196616 | tf_op jit(solution)/shard_map/ppermute | solution.py:288
  47.6 0.7 %project.1 = (bf16[4,2,128,512]{3,2,1,0:T(8,128)(2,1)S(1)}, bf16[4,2,512,128]{3,2,1,0:T(8,128)(2,1)S(1)}) custom-call(bf16[4,2,128,128]{3,2,1,0:T(8,128)(2,1)S(1)} %pad_maximum_fusion.refs_0_, bf16[4,2,128,128]{3,2,1,0:T(8,128)(2,1)S(1)} %collective-permute-done.5.refs_1_, bf16[4,2,128,128]{3,2,1,0:T(8,128)(2,1)S(1)} %collective-permute-done.6.refs_2_, ...), custom_call_target="tpu_custom_call" | custom-call | flops 268435456 | bytes 3145728 | tf_op jit(solution)/shard_map/project/pallas_call | solution.py:171
  48.3 3.7 %collective-permute-start.16 = (bf16[2,128,128]{2,1,0:T(8,128)(2,1)S(1)}, bf16[2,128,128]{2,1,0:T(8,128)(2,1)S(1)}, u32[]{:S(2)}, u32[]{:S(2)}) collective-permute-start(bf16[2,128,128]{2,1,0:T(8,128)(2,1)S(1)} %collective-permute-done), channel_id=1, source_target_pairs={{0,0},{1,1},{2,2},{3,3},{4,64},{5,65},{6,66},{7,67},{8,128},{9,129... | collective-permute-start | bytes 196616 | tf_op jit(solution)/shard_map/ppermute | solution.py:288
  52.1 1.2 %shard_map.118 = bf16[2,144,128]{2,1,0:T(8,128)(2,1)S(1)} custom-call(bf16[2,128,128]{2,1,0:T(8,128)(2,1)S(1)} %collective-permute-done.1.rows, bf16[4,2,128,512]{3,2,1,0:T(8,128)(2,1)S(1)} %get-tuple-element.7.keys, bf16[4,2,512,128]{3,2,1,0:T(8,128)(2,1)S(1)} %get-tuple-element.8.values, f32[4,128,128]{2,1,0:T(8,128)S(1)} %copy-done, ...), custom_call_target="tpu_custom_call" | custom-call | flops 268435456 | bytes 2097152 | tf_op jit(solution)/shard_map/pallas_call | solution.py:222
  53.3 2.7 %collective-permute-start.11 = (bf16[2,144,128]{2,1,0:T(8,128)(2,1)S(1)}, bf16[2,144,128]{2,1,0:T(8,128)(2,1)S(1)}, u32[]{:S(2)}, u32[]{:S(2)}) collective-permute-start(bf16[2,144,128]{2,1,0:T(8,128)(2,1)S(1)} %shard_map.118), channel_id=1, source_target_pairs={{0,8},{1,9},{2,10},{3,11},{4,12},{5,13},{6,14},{7,15},{8,0},{9,1},... | collective-permute-start | bytes 221192 | tf_op jit(solution)/shard_map/ppermute | solution.py:288
  56.1 1.2 %shard_map.119 = bf16[2,144,128]{2,1,0:T(8,128)(2,1)S(1)} custom-call(bf16[2,128,128]{2,1,0:T(8,128)(2,1)S(1)} %collective-permute-done.12.rows, bf16[4,2,128,512]{3,2,1,0:T(8,128)(2,1)S(1)} %get-tuple-element.7.keys, bf16[4,2,512,128]{3,2,1,0:T(8,128)(2,1)S(1)} %get-tuple-element.8.values, f32[4,128,128]{2,1,0:T(8,128)S(1)} %copy-done, ...), custom_call_target="tpu_custom_call" | custom-call | flops 268435456 | bytes 2097152 | tf_op jit(solution)/shard_map/pallas_call | solution.py:222
  57.3 3.2 %collective-permute-start.13 = (bf16[2,144,128]{2,1,0:T(8,128)(2,1)S(1)}, bf16[2,144,128]{2,1,0:T(8,128)(2,1)S(1)}, u32[]{:S(2)}, u32[]{:S(2)}) collective-permute-start(bf16[2,144,128]{2,1,0:T(8,128)(2,1)S(1)} %shard_map.119), channel_id=1, source_target_pairs={{0,12},{1,13},{2,14},{3,15},{4,0},{5,1},{6,2},{7,3},{8,4},{9,5},{1... | collective-permute-start | bytes 221192 | tf_op jit(solution)/shard_map/ppermute | solution.py:288
  60.5 1.2 %shard_map.120 = bf16[2,144,128]{2,1,0:T(8,128)(2,1)S(1)} custom-call(bf16[2,128,128]{2,1,0:T(8,128)(2,1)S(1)} %collective-permute-done.14.rows, bf16[4,2,128,512]{3,2,1,0:T(8,128)(2,1)S(1)} %get-tuple-element.7.keys, bf16[4,2,512,128]{3,2,1,0:T(8,128)(2,1)S(1)} %get-tuple-element.8.values, f32[4,128,128]{2,1,0:T(8,128)S(1)} %copy-done, ...), custom_call_target="tpu_custom_call" | custom-call | flops 268435456 | bytes 2097152 | tf_op jit(solution)/shard_map/pallas_call | solution.py:222
  61.7 0.1 collective-permute-start.15
  61.7 1.2 %shard_map.121.fourth = bf16[2,144,128]{2,1,0:T(8,128)(2,1)S(1)} custom-call(bf16[2,128,128]{2,1,0:T(8,128)(2,1)S(1)} %collective-permute-done.16.rows, bf16[4,2,128,512]{3,2,1,0:T(8,128)(2,1)S(1)} %get-tuple-element.7.keys, bf16[4,2,512,128]{3,2,1,0:T(8,128)(2,1)S(1)} %get-tuple-element.8.values, f32[4,128,128]{2,1,0:T(8,128)S(1)} %copy-done, ...), custom_call_target="tpu_custom_call" | custom-call | flops 268435456 | bytes 2097152 | tf_op jit(solution)/shard_map/pallas_call | solution.py:222
  63.0 4.3 %collective-permute-done.15.third = bf16[2,144,128]{2,1,0:T(8,128)(2,1)S(1)} collective-permute-done((bf16[2,144,128]{2,1,0:T(8,128)(2,1)S(1)}, bf16[2,144,128]{2,1,0:T(8,128)(2,1)S(1)}, u32[]{:S(2)}, u32[]{:S(2)}) %collective-permute-start.15) | collective-permute-done | bytes 73760 | tf_op jit(solution)/shard_map/ppermute | solution.py:288
  67.3 1.2 %finish.1 = bf16[2,128,128]{2,1,0:T(8,128)(2,1)} custom-call(bf16[2,144,128]{2,1,0:T(8,128)(2,1)S(1)} %collective-permute-done.11.first, bf16[2,144,128]{2,1,0:T(8,128)(2,1)S(1)} %collective-permute-done.13.second, bf16[2,144,128]{2,1,0:T(8,128)(2,1)S(1)} %collective-permute-done.15.third, bf16[2,144,128]{2,1,0:T(8,128)(2,1)S(1)} %shard_map.121.fourth, ...), custom_call_target="tpu_custom_call" | custom-call | flops 16777216 | bytes 524288 | tf_op jit(solution)/shard_map/finish/pallas_call | solution.py:267
  (25 shorter events, 0.1 us)
Async XLA Ops:
  0.0 47.6 %copy-start.2 = (bf16[128,128]{1,0:T(8,128)(2,1)S(1)}, bf16[128,128]{1,0:T(8,128)(2,1)}, u32[]{:S(2)}) copy-start(bf16[128,128]{1,0:T(8,128)(2,1)} %refs_4_.1) | copy-start | bytes 98308
  0.0 47.6 %copy-start.3 = (bf16[128,128]{1,0:T(8,128)(2,1)S(1)}, bf16[128,128]{1,0:T(8,128)(2,1)}, u32[]{:S(2)}) copy-start(bf16[128,128]{1,0:T(8,128)(2,1)} %refs_5_.1) | copy-start | bytes 98308
  0.0 52.1 %copy-start.1 = (bf16[128,128]{1,0:T(8,128)(2,1)S(1)}, bf16[128,128]{1,0:T(8,128)(2,1)}, u32[]{:S(2)}) copy-start(bf16[128,128]{1,0:T(8,128)(2,1)} %w_query.7) | copy-start | bytes 98308
  7.4 23.8 %copy-start = (f32[4,128,128]{2,1,0:T(8,128)S(1)}, f32[4,128,128]{2,1,0:T(8,128)}, u32[]{:S(2)}) copy-start(f32[4,128,128]{2,1,0:T(8,128)} %pair_bias.1.bias_a) | copy-start | bytes 786436
  7.4 23.8 %collective-permute-start.8 = (f32[4,128,128]{2,1,0:T(8,128)}, f32[4,128,128]{2,1,0:T(8,128)S(1)}, u32[]{:S(2)}, u32[]{:S(2)}) collective-permute-start(f32[4,128,128]{2,1,0:T(8,128)} %pair_bias.1.bias_a), channel_id=1, source_target_pairs={{0,2},{1,3},{2,0},{3,1},{4,6},{5,7},{6,4},{7,5},{8,10},{9,11},{10,... | collective-permute-start | bytes 786440 | tf_op jit(solution)/shard_map/ppermute | solution.py:288
  11.9 13.6 %collective-permute-start = (bf16[2,128,128]{2,1,0:T(8,128)(2,1)}, bf16[2,128,128]{2,1,0:T(8,128)(2,1)S(1)}, u32[]{:S(2)}, u32[]{:S(2)}) collective-permute-start(bf16[2,128,128]{2,1,0:T(8,128)(2,1)} %fetch.1), channel_id=1, source_target_pairs={{0,0},{1,16},{2,32},{3,48},{4,4},{5,20},{6,36},{7,52},{8,8},{9,24}... | collective-permute-start | bytes 196616 | tf_op jit(solution)/shard_map/ppermute | solution.py:288
  13.4 12.1 %collective-permute-start.4 = (bf16[2,128,128]{2,1,0:T(8,128)(2,1)}, bf16[2,128,128]{2,1,0:T(8,128)(2,1)S(1)}, u32[]{:S(2)}, u32[]{:S(2)}) collective-permute-start(bf16[2,128,128]{2,1,0:T(8,128)(2,1)} %fetch.1), channel_id=1, source_target_pairs={{0,48},{1,0},{2,16},{3,32},{4,52},{5,4},{6,20},{7,36},{8,56},{9,8}... | collective-permute-start | bytes 196616 | tf_op jit(solution)/shard_map/ppermute | solution.py:288
  19.3 8.2 %collective-permute-start.3 = (bf16[2,128,128]{2,1,0:T(8,128)(2,1)}, bf16[2,128,128]{2,1,0:T(8,128)(2,1)S(1)}, u32[]{:S(2)}, u32[]{:S(2)}) collective-permute-start(bf16[2,128,128]{2,1,0:T(8,128)(2,1)} %fetch.1), channel_id=1, source_target_pairs={{0,32},{1,48},{2,0},{3,16},{4,36},{5,52},{6,4},{7,20},{8,40},{9,56... | collective-permute-start | bytes 196616 | tf_op jit(solution)/shard_map/ppermute | solution.py:288
  22.7 5.5 %collective-permute-start.2 = (bf16[2,128,128]{2,1,0:T(8,128)(2,1)}, bf16[2,128,128]{2,1,0:T(8,128)(2,1)S(1)}, u32[]{:S(2)}, u32[]{:S(2)}) collective-permute-start(bf16[2,128,128]{2,1,0:T(8,128)(2,1)} %fetch.1), channel_id=1, source_target_pairs={{0,16},{1,32},{2,48},{3,0},{4,20},{5,36},{6,52},{7,4},{8,24},{9,40... | collective-permute-start | bytes 196616 | tf_op jit(solution)/shard_map/ppermute | solution.py:288
  28.3 9.3 %collective-permute-start.5 = (bf16[4,2,128,128]{3,2,1,0:T(8,128)(2,1)S(1)}, bf16[4,2,128,128]{3,2,1,0:T(8,128)(2,1)S(1)}, u32[]{:S(2)}, u32[]{:S(2)}) collective-permute-start(bf16[4,2,128,128]{3,2,1,0:T(8,128)(2,1)S(1)} %pad_maximum_fusion.refs_0_), channel_id=1, source_target_pairs={{0,64},{1,65},{2,66},{3,67},{4,68},{5,69},{6,70},{7,71},{8,72},{9,... | collective-permute-start | bytes 786440 | tf_op jit(solution)/shard_map/ppermute | solution.py:288
  28.6 10.7 %collective-permute-start.6 = (bf16[4,2,128,128]{3,2,1,0:T(8,128)(2,1)S(1)}, bf16[4,2,128,128]{3,2,1,0:T(8,128)(2,1)S(1)}, u32[]{:S(2)}, u32[]{:S(2)}) collective-permute-start(bf16[4,2,128,128]{3,2,1,0:T(8,128)(2,1)S(1)} %pad_maximum_fusion.refs_0_), channel_id=1, source_target_pairs={{0,128},{1,129},{2,130},{3,131},{4,132},{5,133},{6,134},{7,135},{8... | collective-permute-start | bytes 786440 | tf_op jit(solution)/shard_map/ppermute | solution.py:288
  31.2 14.6 %collective-permute-start.7 = (bf16[4,2,128,128]{3,2,1,0:T(8,128)(2,1)S(1)}, bf16[4,2,128,128]{3,2,1,0:T(8,128)(2,1)S(1)}, u32[]{:S(2)}, u32[]{:S(2)}) collective-permute-start(bf16[4,2,128,128]{3,2,1,0:T(8,128)(2,1)S(1)} %pad_maximum_fusion.refs_0_), channel_id=1, source_target_pairs={{0,192},{1,193},{2,194},{3,195},{4,196},{5,197},{6,198},{7,199},{8... | collective-permute-start | bytes 786440 | tf_op jit(solution)/shard_map/ppermute | solution.py:288
  31.2 20.9 %collective-permute-start.9 = (f32[4,128,128]{2,1,0:T(8,128)S(1)}, f32[4,128,128]{2,1,0:T(8,128)S(1)}, u32[]{:S(2)}, u32[]{:S(2)}) collective-permute-start(f32[4,128,128]{2,1,0:T(8,128)S(1)} %copy-done), channel_id=1, source_target_pairs={{0,1},{1,0},{2,3},{3,2},{4,5},{5,4},{6,7},{7,6},{8,9},{9,8},{10,11... | collective-permute-start | bytes 786440 | tf_op jit(solution)/shard_map/ppermute | solution.py:288
  31.2 20.8 %collective-permute-start.10 = (f32[4,128,128]{2,1,0:T(8,128)S(1)}, f32[4,128,128]{2,1,0:T(8,128)S(1)}, u32[]{:S(2)}, u32[]{:S(2)}) collective-permute-start(f32[4,128,128]{2,1,0:T(8,128)S(1)} %collective-permute-done.8.bias_b), channel_id=1, source_target_pairs={{0,1},{1,0},{2,3},{3,2},{4,5},{5,4},{6,7},{7,6},{8,9},{9,8},{10,11... | collective-permute-start | bytes 786440 | tf_op jit(solution)/shard_map/ppermute | solution.py:288
  37.6 10.8 %collective-permute-start.1 = (bf16[2,128,128]{2,1,0:T(8,128)(2,1)S(1)}, bf16[2,128,128]{2,1,0:T(8,128)(2,1)S(1)}, u32[]{:S(2)}, u32[]{:S(2)}) collective-permute-start(bf16[2,128,128]{2,1,0:T(8,128)(2,1)S(1)} %collective-permute-done), channel_id=1, source_target_pairs={{0,8},{1,9},{2,10},{3,11},{4,72},{5,73},{6,74},{7,75},{8,136},{9,1... | collective-permute-start | bytes 196616 | tf_op jit(solution)/shard_map/ppermute | solution.py:288
  39.4 16.7 %collective-permute-start.12 = (bf16[2,128,128]{2,1,0:T(8,128)(2,1)S(1)}, bf16[2,128,128]{2,1,0:T(8,128)(2,1)S(1)}, u32[]{:S(2)}, u32[]{:S(2)}) collective-permute-start(bf16[2,128,128]{2,1,0:T(8,128)(2,1)S(1)} %collective-permute-done), channel_id=1, source_target_pairs={{0,4},{1,5},{2,6},{3,7},{4,68},{5,69},{6,70},{7,71},{8,132},{9,133... | collective-permute-start | bytes 196616 | tf_op jit(solution)/shard_map/ppermute | solution.py:288
  45.8 14.7 %collective-permute-start.14 = (bf16[2,128,128]{2,1,0:T(8,128)(2,1)S(1)}, bf16[2,128,128]{2,1,0:T(8,128)(2,1)S(1)}, u32[]{:S(2)}, u32[]{:S(2)}) collective-permute-start(bf16[2,128,128]{2,1,0:T(8,128)(2,1)S(1)} %collective-permute-done), channel_id=1, source_target_pairs={{0,12},{1,13},{2,14},{3,15},{4,76},{5,77},{6,78},{7,79},{8,140},{9... | collective-permute-start | bytes 196616 | tf_op jit(solution)/shard_map/ppermute | solution.py:288
  48.3 13.4 %collective-permute-start.16 = (bf16[2,128,128]{2,1,0:T(8,128)(2,1)S(1)}, bf16[2,128,128]{2,1,0:T(8,128)(2,1)S(1)}, u32[]{:S(2)}, u32[]{:S(2)}) collective-permute-start(bf16[2,128,128]{2,1,0:T(8,128)(2,1)S(1)} %collective-permute-done), channel_id=1, source_target_pairs={{0,0},{1,1},{2,2},{3,3},{4,64},{5,65},{6,66},{7,67},{8,128},{9,129... | collective-permute-start | bytes 196616 | tf_op jit(solution)/shard_map/ppermute | solution.py:288
  53.3 14.0 %copy-start.4 = (bf16[128,128]{1,0:T(8,128)(2,1)S(1)}, bf16[128,128]{1,0:T(8,128)(2,1)}, u32[]{:S(2)}) copy-start(bf16[128,128]{1,0:T(8,128)(2,1)} %w_gate.1) | copy-start | bytes 98308
  53.3 14.0 %copy-start.5 = (bf16[128,128]{1,0:T(8,128)(2,1)S(1)}, bf16[128,128]{1,0:T(8,128)(2,1)}, u32[]{:S(2)}) copy-start(bf16[128,128]{1,0:T(8,128)(2,1)} %w_out.1) | copy-start | bytes 98308
  53.3 14.0 %copy-start.6 = (f32[128]{0:T(128)S(1)}, f32[128]{0:T(128)}, u32[]{:S(2)}) copy-start(f32[128]{0:T(128)} %param.21) | copy-start | bytes 1540
  53.3 9.6 %collective-permute-start.11 = (bf16[2,144,128]{2,1,0:T(8,128)(2,1)S(1)}, bf16[2,144,128]{2,1,0:T(8,128)(2,1)S(1)}, u32[]{:S(2)}, u32[]{:S(2)}) collective-permute-start(bf16[2,144,128]{2,1,0:T(8,128)(2,1)S(1)} %shard_map.118), channel_id=1, source_target_pairs={{0,8},{1,9},{2,10},{3,11},{4,12},{5,13},{6,14},{7,15},{8,0},{9,1},... | collective-permute-start | bytes 221192 | tf_op jit(solution)/shard_map/ppermute | solution.py:288
  57.3 5.7 %collective-permute-start.13 = (bf16[2,144,128]{2,1,0:T(8,128)(2,1)S(1)}, bf16[2,144,128]{2,1,0:T(8,128)(2,1)S(1)}, u32[]{:S(2)}, u32[]{:S(2)}) collective-permute-start(bf16[2,144,128]{2,1,0:T(8,128)(2,1)S(1)} %shard_map.119), channel_id=1, source_target_pairs={{0,12},{1,13},{2,14},{3,15},{4,0},{5,1},{6,2},{7,3},{8,4},{9,5},{1... | collective-permute-start | bytes 221192 | tf_op jit(solution)/shard_map/ppermute | solution.py:288
  61.7 5.6 %collective-permute-start.15 = (bf16[2,144,128]{2,1,0:T(8,128)(2,1)S(1)}, bf16[2,144,128]{2,1,0:T(8,128)(2,1)S(1)}, u32[]{:S(2)}, u32[]{:S(2)}) collective-permute-start(bf16[2,144,128]{2,1,0:T(8,128)(2,1)S(1)} %shard_map.120), channel_id=1, source_target_pairs={{0,4},{1,5},{2,6},{3,7},{4,8},{5,9},{6,10},{7,11},{8,12},{9,13},{1... | collective-permute-start | bytes 221192 | tf_op jit(solution)/shard_map/ppermute | solution.py:288
where the time goes:
time: 68.7 us; the launch traced here: 68.5 us
  starting transfers between devices  38.1 us (55%)
  Pallas kernels  16.7 us (24%)
  waiting for transfers between devices  13.5 us (20%)
    ppermute x17, starting transfers between devices, send(): return lax.ppermute(value, AXES, moves(target))  38.1 us
    ppermute x17, waiting for transfers between devices, send(): return lax.ppermute(value, AXES, moves(target))  13.5 us
    pallas_call x1, Pallas kernels, pair_bias(): pl.pallas_call(bias_kernel, in_specs=[pl.BlockSpec(memory_space=pltpu.HBM...  7.41 us
    pallas_call x4, Pallas kernels, attend(): pl.pallas_call(attend_kernel, grid=(1,), in_specs=[full[0], *parts, *full...  4.88 us
    pallas_call x1, Pallas kernels, fetch(): pl.pallas_call(fetch_kernel, in_specs=[pl.BlockSpec(memory_space=pltpu.HB...  2.46 us
  transfers between devices with their start and end apart: 17, of which 5 were waited for; matrix products, arithmetic and copies ran while one was open for 0% of the time, Pallas kernels for 12%

commit v1 on v0

--- a/solution.py
+++ b/solution.py
@@ -1,3 +1,5 @@
+import functools
+
 import jax
 import jax.numpy as jnp
 from jax import lax
@@ -100,20 +102,23 @@
         value = jnp.broadcast_to(value[:, None], (heads, 8, width)).reshape(heads * 8, width)
         for j in range(8):
             placed = jnp.where(at == j, value, 0.0).astype(BF16)
-            lifted[j, part * heads * 8 : (part + 1) * heads * 8] = placed
+            at_j = slice(j * width, (j + 1) * width)
+            lifted[part * heads * 8 : (part + 1) * heads * 8, at_j] = placed
     real = live[...] > 0
     sub = lax.broadcasted_iota(jnp.int32, (8, tokens), 0)
 
     def eight(group, carry):
-        total = jnp.zeros((2 * heads * 8, tokens), F32)
         spread = jnp.zeros((8, tokens), F32)
+        turned = []
         for j in range(8):
             values = rows[group * 8 + j].T.astype(F32)
             values = values - jnp.sum(values, axis=0, keepdims=True) * (1.0 / width)
-            total += jnp.dot(lifted[j], values.astype(BF16), preferred_element_type=F32)
+            turned.append(values.astype(BF16))
             squares = jnp.sum(values * values, axis=0, keepdims=True)
             spread = jnp.where(sub == j, squares, spread)
         scale = lax.rsqrt(spread * (1.0 / width) + 1e-05)
+        turned = jnp.concatenate(turned, axis=0)
+        total = jnp.dot(lifted[...], turned, preferred_element_type=F32)
         total = total[: heads * 8] + total[heads * 8 :]
         total = total.reshape(heads, 8, tokens) * scale[None] + offset
         out[:, pl.ds(pl.multiple_of(group * 8, 8), 8), :] = jnp.where(real, total, MASKED)
@@ -134,7 +139,7 @@
         out_shape=jax.ShapeDtypeStruct((heads, block, tokens), F32),
         scratch_shapes=[
             VMEM((block, tokens, width), BF16),
-            VMEM((8, 2 * heads * 8, width), BF16),
+            VMEM((2 * heads * 8, 8 * width), BF16),
             VMEM((1, width), F32),
             VMEM((1, width), F32),
             VMEM((heads, width), BF16),
@@ -148,7 +153,9 @@
 
 
 def project_kernel(*refs):
-    blocks, (w_key, w_value, keys, values) = refs[:-4], refs[-4:]
+    blocks, (w_key, w_value, bias, keys, values, bias_near, sem) = refs[:4], refs[4:]
+    copy = pltpu.make_async_copy(bias, bias_near, sem)
+    copy.start()
     block, width = blocks[0].shape[-2:]
     row, col = lax.axis_index("row"), lax.axis_index("col")
     y, h, x, q = row // 4, row % 4, col // 4, col % 4
@@ -164,34 +171,43 @@
                 at = pl.ds(pl.multiple_of(places[4 + i] * block, block), block)
                 keys[places[s], t, :, at] = both[:, :width].T
                 values[places[s], t, at, :] = both[:, width:]
-
-
-def project(blocks, w_key, w_value):
+    copy.wait()
+
+
+def project(blocks, w_key, w_value, bias):
     block, width = blocks[0].shape[-2:]
     return pl.pallas_call(
         project_kernel,
-        in_specs=[whole()] * (len(blocks) + 2),
-        out_specs=[whole(), whole()],
+        in_specs=[whole()] * 6 + [pl.BlockSpec(memory_space=pltpu.HBM)],
+        out_specs=[whole()] * 3,
         out_shape=[
             jax.ShapeDtypeStruct((4, 2, width, 4 * block), BF16),
             jax.ShapeDtypeStruct((4, 2, 4 * block, width), BF16),
+            jax.ShapeDtypeStruct(bias.shape, F32),
         ],
+        scratch_shapes=[pltpu.SemaphoreType.DMA],
         compiler_params=params(),
         cost_estimate=cost(2 * 4096 * 128 * 256, 3 << 20),
         name="project",
-    )(*blocks, w_key, w_value)
-
-
-def attend_kernel(rows, keys, values, bias_a, bias_b, bias_c, bias_d, w_query, out):
+    )(*blocks, w_key, w_value, bias)
+
+
+def attend_kernel(v, rows, keys, values, bias_a, bias_b, bias_c, bias_d, w_query, *rest):
     block, width = rows.shape[1:]
     heads = bias_a.shape[0]
     head_dim = width // heads
     lane = lax.broadcasted_iota(jnp.int32, (block, width), 1)
+    out = rest[-1]
+    if len(rest) > 1:
+        w_gate, gate_bias, gates, out = rest
+        for t in range(2):
+            gate = jnp.dot(rows[t], w_gate[...], preferred_element_type=F32) + gate_bias[...]
+            gates[t] = jax.nn.sigmoid(gate).astype(BF16)
     for t in range(2):
         query = jnp.dot(rows[t], w_query[...], preferred_element_type=F32)
         query = (query * (head_dim**-0.5)).astype(BF16)
-        key = keys[0, t]
-        value = jnp.concatenate([values[0, t], jnp.ones((4 * block, width), BF16)], axis=1)
+        key = keys[v, t]
+        value = jnp.concatenate([values[v, t], jnp.ones((4 * block, width), BF16)], axis=1)
         summed = jnp.zeros((block, width), F32)
         stats = jnp.zeros((block, width), F32)
         for h in range(heads):
@@ -213,25 +229,23 @@
         out[t, block:] = stats.T[:STATS].astype(BF16)
 
 
-def attend(s, rows, keys, values, biases, w_query):
+def attend(v, rows, keys, values, biases, w_query, gating=()):
     _, block, width = rows.shape
-    parts = [pl.BlockSpec((1, *v.shape[1:]), lambda i: (s, 0, 0, 0)) for v in (keys, values)]
-    full = [
-        pl.BlockSpec(v.shape, lambda i, n=v.ndim: (0,) * n) for v in (rows, *biases, w_query)
-    ]
-    return pl.pallas_call(
-        attend_kernel,
-        grid=(1,),
-        in_specs=[full[0], *parts, *full[1:]],
-        out_specs=pl.BlockSpec((2, block + STATS, width), lambda i: (0, 0, 0)),
-        out_shape=jax.ShapeDtypeStruct((2, block + STATS, width), BF16),
+    shapes = [jax.ShapeDtypeStruct((2, block + STATS, width), BF16)]
+    if gating:
+        shapes.insert(0, jax.ShapeDtypeStruct(rows.shape, BF16))
+    return pl.pallas_call(
+        functools.partial(attend_kernel, v),
+        in_specs=[whole()] * (8 + len(gating)),
+        out_specs=[whole()] * len(shapes),
+        out_shape=shapes,
         compiler_params=params(),
         cost_estimate=cost(8 * 2 * 128 * 512 * 128 * 2, 2 << 20, 2 * 4 * 128 * 512),
-    )(rows, keys, values, *biases, w_query)
-
-
-def finish_kernel(first, second, third, fourth, rows, w_gate, gate_bias, w_out, out):
-    block, width = rows.shape[1:]
+    )(rows, keys, values, *biases, w_query, *gating)
+
+
+def finish_kernel(first, second, third, fourth, gates, w_out, out):
+    block, width = gates.shape[1:]
     heads = STATS // 4
     head_dim = width // heads
     parts = (first, second, third, fourth)
@@ -257,22 +271,20 @@
         attended = jnp.zeros((block, width), F32)
         for p, part in enumerate(parts):
             attended += wide[:, p * width : (p + 1) * width] * part[t, :block].astype(F32)
-        gate = jnp.dot(rows[t], w_gate[...], preferred_element_type=F32) + gate_bias[...]
-        gate = jax.nn.sigmoid(gate).astype(BF16).astype(F32)
-        gated = (gate * attended).astype(BF16)
+        gated = (gates[t].astype(F32) * attended).astype(BF16)
         out[t] = jnp.dot(gated, w_out[...], preferred_element_type=F32).astype(BF16)
 
 
-def finish(parts, rows, w_gate, gate_bias, w_out):
+def finish(parts, gates, w_out):
     return pl.pallas_call(
         finish_kernel,
-        in_specs=[whole()] * 8,
+        in_specs=[whole()] * 6,
         out_specs=whole(),
-        out_shape=jax.ShapeDtypeStruct(rows.shape, BF16),
+        out_shape=jax.ShapeDtypeStruct(gates.shape, BF16),
         compiler_params=params(),
         cost_estimate=cost(4 * 256 * 128 * 128, 1 << 19),
         name="finish",
-    )(*parts, rows, w_gate, gate_bias, w_out)
+    )(*parts, gates, w_out)
 
 
 def moves(target):
@@ -313,7 +325,6 @@
     bias_z = send(bias, lambda y, h, x, q: (y, h, x, q ^ 2))
     bias_c = send(bias, lambda y, h, x, q: (y, h, x, q ^ 1))
     bias_zc = send(bias_z, lambda y, h, x, q: (y, h, x, q ^ 1))
-    biases = (bias, bias_z, bias_c, bias_zc)
 
     own = jnp.stack(low)
     rows_kv = [own]
@@ -323,14 +334,15 @@
     for s in range(4):
         rows_q.append(send(low[0], lambda y, h, x, q, s=s: (x, h, y + s, q)))
 
-    keys, values = project(rows_kv, w_key, w_value)
+    keys, values, bias = project(rows_kv, w_key, w_value, bias)
+    biases = (bias, bias_z, bias_c, bias_zc)
     parts = []
-    for s in (2, 1, 3, 0):
-        part = attend(s, rows_q[s], keys, values, biases, w_query)
-        if s:
-            part = send(part, lambda y, h, x, q, s=s: (y, h, x - s, q))
-        parts.append(part)
-    return finish(parts, rows_q[0], w_gate, gate_bias.reshape(1, width), w_out)
+    for s in (2, 1, 3):
+        (part,) = attend(s, rows_q[s], keys, values, biases, w_query)
+        parts.append(send(part, lambda y, h, x, q, s=s: (y, h, x - s, q)))
+    gating = (w_gate, gate_bias.reshape(1, width))
+    gates, part = attend(0, rows_q[0], keys, values, biases, w_query, gating)
+    return finish(parts + [part], gates, w_out)
 
 
 def solution(mesh):

time: 68.7 us -> 68.6 us (level)
  the two profiles are of different devices: /device:TPU:24 before, /device:TPU:16 now
where the time goes in v1:
time: 68.6 us; the launch traced here: 68.4 us
  starting transfers between devices  32.3 us (47%)
  waiting for transfers between devices  19.2 us (28%)
  Pallas kernels  16.6 us (24%)
    ppermute x17, starting transfers between devices, send(): return lax.ppermute(value, AXES, moves(target))  32.3 us
    ppermute x17, waiting for transfers between devices, send(): return lax.ppermute(value, AXES, moves(target))  19.2 us
    pallas_call x1, Pallas kernels, pair_bias(): pl.pallas_call(bias_kernel, in_specs=[pl.BlockSpec(memory_space=pltpu.HBM...  7.28 us
    pallas_call x4, Pallas kernels, attend(): pl.pallas_call(functools.partial(attend_kernel, v), in_specs=[whole()] *...  4.93 us
    pallas_call x1, Pallas kernels, fetch(): pl.pallas_call(fetch_kernel, in_specs=[pl.BlockSpec(memory_space=pltpu.HB...  2.46 us
  transfers between devices with their start and end apart: 17, of which 5 were waited for; matrix products, arithmetic and copies ran while one was open for 0% of the time, Pallas kernels for 12%

profile of v1, /device:TPU:16, one launch (start us, length us, event | category | flops | bytes accessed | tf_op | source)
XLA Modules:
  0.0 68.4 jit_solution(178464951527869676)
XLA Ops:
  0.0 7.3 %pair_bias.1.refs_6_ = f32[4,128,128]{2,1,0:T(8,128)} custom-call(bf16[128,128,128]{2,1,0:T(8,128)(2,1)} %pair_rep.3, f32[1,128]{1,0:T(1,128)} %bitcast.14, f32[1,128]{1,0:T(1,128)} %bitcast.16, bf16[4,128]{1,0:T(4,128)(2,1)} %bitcast.18, s32[1,128]{1,0:T(1,128)} %bitcast.19), custom_call_target="tpu_custom_call" | custom-call | flops 8388608 | bytes 4194304 | tf_op jit(solution)/shard_map/pair_bias/pallas_call | solution.py:135
  7.3 0.0 copy-start.1
  7.3 2.0 %collective-permute-start.8 = (f32[4,128,128]{2,1,0:T(8,128)}, f32[4,128,128]{2,1,0:T(8,128)S(1)}, u32[]{:S(2)}, u32[]{:S(2)}) collective-permute-start(f32[4,128,128]{2,1,0:T(8,128)} %pair_bias.1.refs_6_), channel_id=1, source_target_pairs={{0,2},{1,3},{2,0},{3,1},{4,6},{5,7},{6,4},{7,5},{8,10},{9,11},{10,... | collective-permute-start | bytes 786440 | tf_op jit(solution)/shard_map/ppermute | solution.py:300
  9.3 2.5 %fetch.1 = bf16[2,128,128]{2,1,0:T(8,128)(2,1)} custom-call(s32[2]{0:T(128)} %row_ids.1, bf16[128,128,128]{2,1,0:T(8,128)(2,1)} %pair_rep.3, f32[1,128]{1,0:T(1,128)} %bitcast.15, f32[1,128]{1,0:T(1,128)} %bitcast.17), custom_call_target="tpu_custom_call" | custom-call | flops 327680 | bytes 131072 | tf_op jit(solution)/shard_map/fetch/pallas_call | solution.py:62
  11.8 1.5 %collective-permute-start = (bf16[2,128,128]{2,1,0:T(8,128)(2,1)}, bf16[2,128,128]{2,1,0:T(8,128)(2,1)S(1)}, u32[]{:S(2)}, u32[]{:S(2)}) collective-permute-start(bf16[2,128,128]{2,1,0:T(8,128)(2,1)} %fetch.1), channel_id=1, source_target_pairs={{0,0},{1,16},{2,32},{3,48},{4,4},{5,20},{6,36},{7,52},{8,8},{9,24}... | collective-permute-start | bytes 196616 | tf_op jit(solution)/shard_map/ppermute | solution.py:300
  13.3 3.8 %collective-permute-start.2 = (bf16[2,128,128]{2,1,0:T(8,128)(2,1)}, bf16[2,128,128]{2,1,0:T(8,128)(2,1)S(1)}, u32[]{:S(2)}, u32[]{:S(2)}) collective-permute-start(bf16[2,128,128]{2,1,0:T(8,128)(2,1)} %fetch.1), channel_id=1, source_target_pairs={{0,16},{1,32},{2,48},{3,0},{4,20},{5,36},{6,52},{7,4},{8,24},{9,40... | collective-permute-start | bytes 196616 | tf_op jit(solution)/shard_map/ppermute | solution.py:300
  17.1 5.4 %collective-permute-start.3 = (bf16[2,128,128]{2,1,0:T(8,128)(2,1)}, bf16[2,128,128]{2,1,0:T(8,128)(2,1)S(1)}, u32[]{:S(2)}, u32[]{:S(2)}) collective-permute-start(bf16[2,128,128]{2,1,0:T(8,128)(2,1)} %fetch.1), channel_id=1, source_target_pairs={{0,32},{1,48},{2,0},{3,16},{4,36},{5,52},{6,4},{7,20},{8,40},{9,56... | collective-permute-start | bytes 196616 | tf_op jit(solution)/shard_map/ppermute | solution.py:300
  22.5 2.9 %collective-permute-start.4 = (bf16[2,128,128]{2,1,0:T(8,128)(2,1)}, bf16[2,128,128]{2,1,0:T(8,128)(2,1)S(1)}, u32[]{:S(2)}, u32[]{:S(2)}) collective-permute-start(bf16[2,128,128]{2,1,0:T(8,128)(2,1)} %fetch.1), channel_id=1, source_target_pairs={{0,48},{1,0},{2,16},{3,32},{4,52},{5,4},{6,20},{7,36},{8,56},{9,8}... | collective-permute-start | bytes 196616 | tf_op jit(solution)/shard_map/ppermute | solution.py:300
  25.4 0.0 collective-permute-done
  25.4 0.7 %collective-permute-done.3 = bf16[2,128,128]{2,1,0:T(8,128)(2,1)S(1)} collective-permute-done((bf16[2,128,128]{2,1,0:T(8,128)(2,1)}, bf16[2,128,128]{2,1,0:T(8,128)(2,1)S(1)}, u32[]{:S(2)}, u32[]{:S(2)}) %collective-permute-start.3) | collective-permute-done | bytes 65568 | tf_op jit(solution)/shard_map/ppermute | solution.py:300
  26.2 1.5 %collective-permute-done.4 = bf16[2,128,128]{2,1,0:T(8,128)(2,1)S(1)} collective-permute-done((bf16[2,128,128]{2,1,0:T(8,128)(2,1)}, bf16[2,128,128]{2,1,0:T(8,128)(2,1)S(1)}, u32[]{:S(2)}, u32[]{:S(2)}) %collective-permute-start.4) | collective-permute-done | bytes 65568 | tf_op jit(solution)/shard_map/ppermute | solution.py:300
  27.7 1.4 %collective-permute-start.5 = (bf16[4,2,128,128]{3,2,1,0:T(8,128)(2,1)S(1)}, bf16[4,2,128,128]{3,2,1,0:T(8,128)(2,1)S(1)}, u32[]{:S(2)}, u32[]{:S(2)}) collective-permute-start(bf16[4,2,128,128]{3,2,1,0:T(8,128)(2,1)S(1)} %pad_maximum_fusion.refs_0_), channel_id=1, source_target_pairs={{0,64},{1,65},{2,66},{3,67},{4,68},{5,69},{6,70},{7,71},{8,72},{9,... | collective-permute-start | bytes 786440 | tf_op jit(solution)/shard_map/ppermute | solution.py:300
  29.0 0.6 collective-permute-start.6
  29.7 1.1 %collective-permute-start.7 = (bf16[4,2,128,128]{3,2,1,0:T(8,128)(2,1)S(1)}, bf16[4,2,128,128]{3,2,1,0:T(8,128)(2,1)S(1)}, u32[]{:S(2)}, u32[]{:S(2)}) collective-permute-start(bf16[4,2,128,128]{3,2,1,0:T(8,128)(2,1)S(1)} %pad_maximum_fusion.refs_0_), channel_id=1, source_target_pairs={{0,192},{1,193},{2,194},{3,195},{4,196},{5,197},{6,198},{7,199},{8... | collective-permute-start | bytes 786440 | tf_op jit(solution)/shard_map/ppermute | solution.py:300
  30.7 0.5 collective-permute-start.10
  31.2 10.9 %collective-permute-done.5.refs_1_ = bf16[4,2,128,128]{3,2,1,0:T(8,128)(2,1)S(1)} collective-permute-done((bf16[4,2,128,128]{3,2,1,0:T(8,128)(2,1)S(1)}, bf16[4,2,128,128]{3,2,1,0:T(8,128)(2,1)S(1)}, u32[]{:S(2)}, u32[]{:S(2)}) %collective-permute-start.5) | collective-permute-done | bytes 262176 | tf_op jit(solution)/shard_map/ppermute | solution.py:300
  42.1 4.3 %collective-permute-start.12 = (bf16[2,128,128]{2,1,0:T(8,128)(2,1)S(1)}, bf16[2,128,128]{2,1,0:T(8,128)(2,1)S(1)}, u32[]{:S(2)}, u32[]{:S(2)}) collective-permute-start(bf16[2,128,128]{2,1,0:T(8,128)(2,1)S(1)} %collective-permute-done), channel_id=1, source_target_pairs={{0,4},{1,5},{2,6},{3,7},{4,68},{5,69},{6,70},{7,71},{8,132},{9,133... | collective-permute-start | bytes 196616 | tf_op jit(solution)/shard_map/ppermute | solution.py:300
  46.4 0.7 %collective-permute-start.1 = (bf16[2,128,128]{2,1,0:T(8,128)(2,1)S(1)}, bf16[2,128,128]{2,1,0:T(8,128)(2,1)S(1)}, u32[]{:S(2)}, u32[]{:S(2)}) collective-permute-start(bf16[2,128,128]{2,1,0:T(8,128)(2,1)S(1)} %collective-permute-done), channel_id=1, source_target_pairs={{0,8},{1,9},{2,10},{3,11},{4,72},{5,73},{6,74},{7,75},{8,136},{9,1... | collective-permute-start | bytes 196616 | tf_op jit(solution)/shard_map/ppermute | solution.py:300
  47.1 0.8 %project.1 = (bf16[4,2,128,512]{3,2,1,0:T(8,128)(2,1)S(1)}, bf16[4,2,512,128]{3,2,1,0:T(8,128)(2,1)S(1)}, f32[4,128,128]{2,1,0:T(8,128)S(1)}) custom-call(bf16[4,2,128,128]{3,2,1,0:T(8,128)(2,1)S(1)} %pad_maximum_fusion.refs_0_, bf16[4,2,128,128]{3,2,1,0:T(8,128)(2,1)S(1)} %collective-permute-done.5.refs_1_, ...), custom_call_target="tpu_custom_call" | custom-call | flops 268435456 | bytes 3145728 | tf_op jit(solution)/shard_map/project/pallas_call | solution.py:179
  47.9 1.5 %collective-permute-done.14.rows = bf16[2,128,128]{2,1,0:T(8,128)(2,1)S(1)} collective-permute-done((bf16[2,128,128]{2,1,0:T(8,128)(2,1)S(1)}, bf16[2,128,128]{2,1,0:T(8,128)(2,1)S(1)}, u32[]{:S(2)}, u32[]{:S(2)}) %collective-permute-start.14) | collective-permute-done | bytes 65568 | tf_op jit(solution)/shard_map/ppermute | solution.py:300
  49.4 4.8 %collective-permute-start.16 = (bf16[2,128,128]{2,1,0:T(8,128)(2,1)S(1)}, bf16[2,128,128]{2,1,0:T(8,128)(2,1)S(1)}, u32[]{:S(2)}, u32[]{:S(2)}) collective-permute-start(bf16[2,128,128]{2,1,0:T(8,128)(2,1)S(1)} %collective-permute-done), channel_id=1, source_target_pairs={{0,0},{1,1},{2,2},{3,3},{4,64},{5,65},{6,66},{7,67},{8,128},{9,129... | collective-permute-start | bytes 196616 | tf_op jit(solution)/shard_map/ppermute | solution.py:300
  54.3 0.0 copy-start.2
  54.3 0.0 copy-start.6
  54.3 1.2 %shard_map.120 = bf16[2,144,128]{2,1,0:T(8,128)(2,1)S(1)} custom-call(bf16[2,128,128]{2,1,0:T(8,128)(2,1)S(1)} %collective-permute-done.14.rows, bf16[4,2,128,512]{3,2,1,0:T(8,128)(2,1)S(1)} %get-tuple-element.10.keys, bf16[4,2,512,128]{3,2,1,0:T(8,128)(2,1)S(1)} %get-tuple-element.11.values, f32[4,128,128]{2,1,0:T(8,128)S(1)} %get-tuple-element.12.bias_a, ...), custom_call_target="tpu_custom_call" | custom-call | flops 268435456 | bytes 2097152 | tf_op jit(solution)/shard_map/pallas_call | solution.py:237
  55.5 0.1 collective-permute-start.15
  55.6 1.2 %shard_map.119 = bf16[2,144,128]{2,1,0:T(8,128)(2,1)S(1)} custom-call(bf16[2,128,128]{2,1,0:T(8,128)(2,1)S(1)} %collective-permute-done.12.rows, bf16[4,2,128,512]{3,2,1,0:T(8,128)(2,1)S(1)} %get-tuple-element.10.keys, bf16[4,2,512,128]{3,2,1,0:T(8,128)(2,1)S(1)} %get-tuple-element.11.values, f32[4,128,128]{2,1,0:T(8,128)S(1)} %get-tuple-element.12.bias_a, ...), custom_call_target="tpu_custom_call" | custom-call | flops 268435456 | bytes 2097152 | tf_op jit(solution)/shard_map/pallas_call | solution.py:237
  56.8 3.3 %collective-permute-start.13 = (bf16[2,144,128]{2,1,0:T(8,128)(2,1)S(1)}, bf16[2,144,128]{2,1,0:T(8,128)(2,1)S(1)}, u32[]{:S(2)}, u32[]{:S(2)}) collective-permute-start(bf16[2,144,128]{2,1,0:T(8,128)(2,1)S(1)} %shard_map.119), channel_id=1, source_target_pairs={{0,12},{1,13},{2,14},{3,15},{4,0},{5,1},{6,2},{7,3},{8,4},{9,5},{1... | collective-permute-start | bytes 221192 | tf_op jit(solution)/shard_map/ppermute | solution.py:300
  60.1 1.2 %shard_map.118 = bf16[2,144,128]{2,1,0:T(8,128)(2,1)S(1)} custom-call(bf16[2,128,128]{2,1,0:T(8,128)(2,1)S(1)} %collective-permute-done.1.rows, bf16[4,2,128,512]{3,2,1,0:T(8,128)(2,1)S(1)} %get-tuple-element.10.keys, bf16[4,2,512,128]{3,2,1,0:T(8,128)(2,1)S(1)} %get-tuple-element.11.values, f32[4,128,128]{2,1,0:T(8,128)S(1)} %get-tuple-element.12.bias_a, ...), custom_call_target="tpu_custom_call" | custom-call | flops 268435456 | bytes 2097152 | tf_op jit(solution)/shard_map/pallas_call | solution.py:237
  61.3 0.1 collective-permute-start.11
  61.4 1.3 %shard_map.121 = (bf16[2,128,128]{2,1,0:T(8,128)(2,1)S(1)}, bf16[2,144,128]{2,1,0:T(8,128)(2,1)S(1)}) custom-call(bf16[2,128,128]{2,1,0:T(8,128)(2,1)S(1)} %collective-permute-done.16.rows, bf16[4,2,128,512]{3,2,1,0:T(8,128)(2,1)S(1)} %get-tuple-element.10.keys, bf16[4,2,512,128]{3,2,1,0:T(8,128)(2,1)S(1)} %get-tuple-element.11.values, ...), custom_call_target="tpu_custom_call" | custom-call | flops 268435456 | bytes 2097152 | tf_op jit(solution)/shard_map/pallas_call | solution.py:237
  62.7 4.5 %collective-permute-done.11.first = bf16[2,144,128]{2,1,0:T(8,128)(2,1)S(1)} collective-permute-done((bf16[2,144,128]{2,1,0:T(8,128)(2,1)S(1)}, bf16[2,144,128]{2,1,0:T(8,128)(2,1)S(1)}, u32[]{:S(2)}, u32[]{:S(2)}) %collective-permute-start.11) | collective-permute-done | bytes 73760 | tf_op jit(solution)/shard_map/ppermute | solution.py:300
  67.2 1.1 %finish.1 = bf16[2,128,128]{2,1,0:T(8,128)(2,1)} custom-call(bf16[2,144,128]{2,1,0:T(8,128)(2,1)S(1)} %collective-permute-done.11.first, bf16[2,144,128]{2,1,0:T(8,128)(2,1)S(1)} %collective-permute-done.13.second, bf16[2,144,128]{2,1,0:T(8,128)(2,1)S(1)} %collective-permute-done.15.third, bf16[2,144,128]{2,1,0:T(8,128)(2,1)S(1)} %get-tuple-element.13.fourth, ...), custom_call_target="tpu_custom_call" | custom-call | flops 16777216 | bytes 524288 | tf_op jit(solution)/shard_map/finish/pallas_call | solution.py:279
  (25 shorter events, 0.1 us)
Async XLA Ops:
  0.0 47.1 %copy-start.4 = (bf16[128,128]{1,0:T(8,128)(2,1)S(1)}, bf16[128,128]{1,0:T(8,128)(2,1)}, u32[]{:S(2)}) copy-start(bf16[128,128]{1,0:T(8,128)(2,1)} %refs_4_.1) | copy-start | bytes 98308
  0.0 47.1 %copy-start.5 = (bf16[128,128]{1,0:T(8,128)(2,1)S(1)}, bf16[128,128]{1,0:T(8,128)(2,1)}, u32[]{:S(2)}) copy-start(bf16[128,128]{1,0:T(8,128)(2,1)} %refs_5_.1) | copy-start | bytes 98308
  7.3 23.4 %copy-start = (f32[4,128,128]{2,1,0:T(8,128)S(1)}, f32[4,128,128]{2,1,0:T(8,128)}, u32[]{:S(2)}) copy-start(f32[4,128,128]{2,1,0:T(8,128)} %pair_bias.1.refs_6_) | copy-start | bytes 786436
  7.3 47.0 %copy-start.1 = (bf16[128,128]{1,0:T(8,128)(2,1)S(1)}, bf16[128,128]{1,0:T(8,128)(2,1)}, u32[]{:S(2)}) copy-start(bf16[128,128]{1,0:T(8,128)(2,1)} %w_query.7) | copy-start | bytes 98308
  7.3 23.4 %collective-permute-start.8 = (f32[4,128,128]{2,1,0:T(8,128)}, f32[4,128,128]{2,1,0:T(8,128)S(1)}, u32[]{:S(2)}, u32[]{:S(2)}) collective-permute-start(f32[4,128,128]{2,1,0:T(8,128)} %pair_bias.1.refs_6_), channel_id=1, source_target_pairs={{0,2},{1,3},{2,0},{3,1},{4,6},{5,7},{6,4},{7,5},{8,10},{9,11},{10,... | collective-permute-start | bytes 786440 | tf_op jit(solution)/shard_map/ppermute | solution.py:300
  11.8 13.6 %collective-permute-start = (bf16[2,128,128]{2,1,0:T(8,128)(2,1)}, bf16[2,128,128]{2,1,0:T(8,128)(2,1)S(1)}, u32[]{:S(2)}, u32[]{:S(2)}) collective-permute-start(bf16[2,128,128]{2,1,0:T(8,128)(2,1)} %fetch.1), channel_id=1, source_target_pairs={{0,0},{1,16},{2,32},{3,48},{4,4},{5,20},{6,36},{7,52},{8,8},{9,24}... | collective-permute-start | bytes 196616 | tf_op jit(solution)/shard_map/ppermute | solution.py:300
  13.3 12.1 %collective-permute-start.2 = (bf16[2,128,128]{2,1,0:T(8,128)(2,1)}, bf16[2,128,128]{2,1,0:T(8,128)(2,1)S(1)}, u32[]{:S(2)}, u32[]{:S(2)}) collective-permute-start(bf16[2,128,128]{2,1,0:T(8,128)(2,1)} %fetch.1), channel_id=1, source_target_pairs={{0,16},{1,32},{2,48},{3,0},{4,20},{5,36},{6,52},{7,4},{8,24},{9,40... | collective-permute-start | bytes 196616 | tf_op jit(solution)/shard_map/ppermute | solution.py:300
  17.1 9.1 %collective-permute-start.3 = (bf16[2,128,128]{2,1,0:T(8,128)(2,1)}, bf16[2,128,128]{2,1,0:T(8,128)(2,1)S(1)}, u32[]{:S(2)}, u32[]{:S(2)}) collective-permute-start(bf16[2,128,128]{2,1,0:T(8,128)(2,1)} %fetch.1), channel_id=1, source_target_pairs={{0,32},{1,48},{2,0},{3,16},{4,36},{5,52},{6,4},{7,20},{8,40},{9,56... | collective-permute-start | bytes 196616 | tf_op jit(solution)/shard_map/ppermute | solution.py:300
  22.5 5.1 %collective-permute-start.4 = (bf16[2,128,128]{2,1,0:T(8,128)(2,1)}, bf16[2,128,128]{2,1,0:T(8,128)(2,1)S(1)}, u32[]{:S(2)}, u32[]{:S(2)}) collective-permute-start(bf16[2,128,128]{2,1,0:T(8,128)(2,1)} %fetch.1), channel_id=1, source_target_pairs={{0,48},{1,0},{2,16},{3,32},{4,52},{5,4},{6,20},{7,36},{8,56},{9,8}... | collective-permute-start | bytes 196616 | tf_op jit(solution)/shard_map/ppermute | solution.py:300
  27.7 14.5 %collective-permute-start.5 = (bf16[4,2,128,128]{3,2,1,0:T(8,128)(2,1)S(1)}, bf16[4,2,128,128]{3,2,1,0:T(8,128)(2,1)S(1)}, u32[]{:S(2)}, u32[]{:S(2)}) collective-permute-start(bf16[4,2,128,128]{3,2,1,0:T(8,128)(2,1)S(1)} %pad_maximum_fusion.refs_0_), channel_id=1, source_target_pairs={{0,64},{1,65},{2,66},{3,67},{4,68},{5,69},{6,70},{7,71},{8,72},{9,... | collective-permute-start | bytes 786440 | tf_op jit(solution)/shard_map/ppermute | solution.py:300
  29.0 13.1 %collective-permute-start.6 = (bf16[4,2,128,128]{3,2,1,0:T(8,128)(2,1)S(1)}, bf16[4,2,128,128]{3,2,1,0:T(8,128)(2,1)S(1)}, u32[]{:S(2)}, u32[]{:S(2)}) collective-permute-start(bf16[4,2,128,128]{3,2,1,0:T(8,128)(2,1)S(1)} %pad_maximum_fusion.refs_0_), channel_id=1, source_target_pairs={{0,128},{1,129},{2,130},{3,131},{4,132},{5,133},{6,134},{7,135},{8... | collective-permute-start | bytes 786440 | tf_op jit(solution)/shard_map/ppermute | solution.py:300
  29.7 16.8 %collective-permute-start.7 = (bf16[4,2,128,128]{3,2,1,0:T(8,128)(2,1)S(1)}, bf16[4,2,128,128]{3,2,1,0:T(8,128)(2,1)S(1)}, u32[]{:S(2)}, u32[]{:S(2)}) collective-permute-start(bf16[4,2,128,128]{3,2,1,0:T(8,128)(2,1)S(1)} %pad_maximum_fusion.refs_0_), channel_id=1, source_target_pairs={{0,192},{1,193},{2,194},{3,195},{4,196},{5,197},{6,198},{7,199},{8... | collective-permute-start | bytes 786440 | tf_op jit(solution)/shard_map/ppermute | solution.py:300
  30.7 23.5 %collective-permute-start.9 = (f32[4,128,128]{2,1,0:T(8,128)S(1)}, f32[4,128,128]{2,1,0:T(8,128)S(1)}, u32[]{:S(2)}, u32[]{:S(2)}) collective-permute-start(f32[4,128,128]{2,1,0:T(8,128)S(1)} %copy-done), channel_id=1, source_target_pairs={{0,1},{1,0},{2,3},{3,2},{4,5},{5,4},{6,7},{7,6},{8,9},{9,8},{10,11... | collective-permute-start | bytes 786440 | tf_op jit(solution)/shard_map/ppermute | solution.py:300
  30.7 23.5 %collective-permute-start.10 = (f32[4,128,128]{2,1,0:T(8,128)S(1)}, f32[4,128,128]{2,1,0:T(8,128)S(1)}, u32[]{:S(2)}, u32[]{:S(2)}) collective-permute-start(f32[4,128,128]{2,1,0:T(8,128)S(1)} %collective-permute-done.8.bias_b), channel_id=1, source_target_pairs={{0,1},{1,0},{2,3},{3,2},{4,5},{5,4},{6,7},{7,6},{8,9},{9,8},{10,11... | collective-permute-start | bytes 786440 | tf_op jit(solution)/shard_map/ppermute | solution.py:300
  42.1 7.3 %collective-permute-start.14 = (bf16[2,128,128]{2,1,0:T(8,128)(2,1)S(1)}, bf16[2,128,128]{2,1,0:T(8,128)(2,1)S(1)}, u32[]{:S(2)}, u32[]{:S(2)}) collective-permute-start(bf16[2,128,128]{2,1,0:T(8,128)(2,1)S(1)} %collective-permute-done), channel_id=1, source_target_pairs={{0,12},{1,13},{2,14},{3,15},{4,76},{5,77},{6,78},{7,79},{8,140},{9... | collective-permute-start | bytes 196616 | tf_op jit(solution)/shard_map/ppermute | solution.py:300
  42.1 13.5 %collective-permute-start.12 = (bf16[2,128,128]{2,1,0:T(8,128)(2,1)S(1)}, bf16[2,128,128]{2,1,0:T(8,128)(2,1)S(1)}, u32[]{:S(2)}, u32[]{:S(2)}) collective-permute-start(bf16[2,128,128]{2,1,0:T(8,128)(2,1)S(1)} %collective-permute-done), channel_id=1, source_target_pairs={{0,4},{1,5},{2,6},{3,7},{4,68},{5,69},{6,70},{7,71},{8,132},{9,133... | collective-permute-start | bytes 196616 | tf_op jit(solution)/shard_map/ppermute | solution.py:300
  46.4 13.7 %collective-permute-start.1 = (bf16[2,128,128]{2,1,0:T(8,128)(2,1)S(1)}, bf16[2,128,128]{2,1,0:T(8,128)(2,1)S(1)}, u32[]{:S(2)}, u32[]{:S(2)}) collective-permute-start(bf16[2,128,128]{2,1,0:T(8,128)(2,1)S(1)} %collective-permute-done), channel_id=1, source_target_pairs={{0,8},{1,9},{2,10},{3,11},{4,72},{5,73},{6,74},{7,75},{8,136},{9,1... | collective-permute-start | bytes 196616 | tf_op jit(solution)/shard_map/ppermute | solution.py:300
  49.4 12.0 %collective-permute-start.16 = (bf16[2,128,128]{2,1,0:T(8,128)(2,1)S(1)}, bf16[2,128,128]{2,1,0:T(8,128)(2,1)S(1)}, u32[]{:S(2)}, u32[]{:S(2)}) collective-permute-start(bf16[2,128,128]{2,1,0:T(8,128)(2,1)S(1)} %collective-permute-done), channel_id=1, source_target_pairs={{0,0},{1,1},{2,2},{3,3},{4,64},{5,65},{6,66},{7,67},{8,128},{9,129... | collective-permute-start | bytes 196616 | tf_op jit(solution)/shard_map/ppermute | solution.py:300
  54.3 7.1 %copy-start.2 = (bf16[128,128]{1,0:T(8,128)(2,1)S(1)}, bf16[128,128]{1,0:T(8,128)(2,1)}, u32[]{:S(2)}) copy-start(bf16[128,128]{1,0:T(8,128)(2,1)} %rest_0_.1) | copy-start | bytes 98308
  54.3 7.1 %copy-start.6 = (f32[128]{0:T(128)S(1)}, f32[128]{0:T(128)}, u32[]{:S(2)}) copy-start(f32[128]{0:T(128)} %param.21) | copy-start | bytes 1540
  55.5 11.7 %copy-start.3 = (bf16[128,128]{1,0:T(8,128)(2,1)S(1)}, bf16[128,128]{1,0:T(8,128)(2,1)}, u32[]{:S(2)}) copy-start(bf16[128,128]{1,0:T(8,128)(2,1)} %w_out.1) | copy-start | bytes 98308
  55.5 7.2 %collective-permute-start.15 = (bf16[2,144,128]{2,1,0:T(8,128)(2,1)S(1)}, bf16[2,144,128]{2,1,0:T(8,128)(2,1)S(1)}, u32[]{:S(2)}, u32[]{:S(2)}) collective-permute-start(bf16[2,144,128]{2,1,0:T(8,128)(2,1)S(1)} %shard_map.120), channel_id=1, source_target_pairs={{0,4},{1,5},{2,6},{3,7},{4,8},{5,9},{6,10},{7,11},{8,12},{9,13},{1... | collective-permute-start | bytes 221192 | tf_op jit(solution)/shard_map/ppermute | solution.py:300
  56.8 5.9 %collective-permute-start.13 = (bf16[2,144,128]{2,1,0:T(8,128)(2,1)S(1)}, bf16[2,144,128]{2,1,0:T(8,128)(2,1)S(1)}, u32[]{:S(2)}, u32[]{:S(2)}) collective-permute-start(bf16[2,144,128]{2,1,0:T(8,128)(2,1)S(1)} %shard_map.119), channel_id=1, source_target_pairs={{0,12},{1,13},{2,14},{3,15},{4,0},{5,1},{6,2},{7,3},{8,4},{9,5},{1... | collective-permute-start | bytes 221192 | tf_op jit(solution)/shard_map/ppermute | solution.py:300
  61.3 5.9 %collective-permute-start.11 = (bf16[2,144,128]{2,1,0:T(8,128)(2,1)S(1)}, bf16[2,144,128]{2,1,0:T(8,128)(2,1)S(1)}, u32[]{:S(2)}, u32[]{:S(2)}) collective-permute-start(bf16[2,144,128]{2,1,0:T(8,128)(2,1)S(1)} %shard_map.118), channel_id=1, source_target_pairs={{0,8},{1,9},{2,10},{3,11},{4,12},{5,13},{6,14},{7,15},{8,0},{9,1},... | collective-permute-start | bytes 221192 | tf_op jit(solution)/shard_map/ppermute | solution.py:300

commit v2 on v1

--- a/solution.py
+++ b/solution.py
@@ -146,16 +146,14 @@
             VMEM((1, tokens), jnp.int32),
             pltpu.SemaphoreType.DMA((4 + block // BIAS_ROWS,)),
         ],
-        compiler_params=params(60),
+        compiler_params=params(52),
         cost_estimate=cost(4 * block * tokens * width, 2 * block * tokens * width),
         name="pair_bias",
     )(pair_rep, ln_gain, ln_bias, w_bias.T, pad_mask.reshape(1, tokens))
 
 
 def project_kernel(*refs):
-    blocks, (w_key, w_value, bias, keys, values, bias_near, sem) = refs[:4], refs[4:]
-    copy = pltpu.make_async_copy(bias, bias_near, sem)
-    copy.start()
+    blocks, (w_key, w_value, keys, values) = refs[:4], refs[4:]
     block, width = blocks[0].shape[-2:]
     row, col = lax.axis_index("row"), lax.axis_index("col")
     y, h, x, q = row // 4, row % 4, col // 4, col % 4
@@ -171,25 +169,22 @@
                 at = pl.ds(pl.multiple_of(places[4 + i] * block, block), block)
                 keys[places[s], t, :, at] = both[:, :width].T
                 values[places[s], t, at, :] = both[:, width:]
-    copy.wait()
-
-
-def project(blocks, w_key, w_value, bias):
+
+
+def project(blocks, w_key, w_value):
     block, width = blocks[0].shape[-2:]
     return pl.pallas_call(
         project_kernel,
-        in_specs=[whole()] * 6 + [pl.BlockSpec(memory_space=pltpu.HBM)],
-        out_specs=[whole()] * 3,
+        in_specs=[whole()] * 6,
+        out_specs=[whole()] * 2,
         out_shape=[
             jax.ShapeDtypeStruct((4, 2, width, 4 * block), BF16),
             jax.ShapeDtypeStruct((4, 2, 4 * block, width), BF16),
-            jax.ShapeDtypeStruct(bias.shape, F32),
         ],
-        scratch_shapes=[pltpu.SemaphoreType.DMA],
         compiler_params=params(),
         cost_estimate=cost(2 * 4096 * 128 * 256, 3 << 20),
         name="project",
-    )(*blocks, w_key, w_value, bias)
+    )(*blocks, w_key, w_value)
 
 
 def attend_kernel(v, rows, keys, values, bias_a, bias_b, bias_c, bias_d, w_query, *rest):
@@ -334,10 +329,10 @@
     for s in range(4):
         rows_q.append(send(low[0], lambda y, h, x, q, s=s: (x, h, y + s, q)))
 
-    keys, values, bias = project(rows_kv, w_key, w_value, bias)
+    keys, values = project(rows_kv, w_key, w_value)
     biases = (bias, bias_z, bias_c, bias_zc)
     parts = []
-    for s in (2, 1, 3):
+    for s in (3, 1, 2):
         (part,) = attend(s, rows_q[s], keys, values, biases, w_query)
         parts.append(send(part, lambda y, h, x, q, s=s: (y, h, x - s, q)))
     gating = (w_gate, gate_bias.reshape(1, width))

time: 68.6 us -> 70.7 us (1.031)
  local copies, waits for them, and re-layouts: 0.03 us -> 2.67 us
  Pallas kernels: 16.6 us -> 15.8 us
    unnamed x14 -> x20, local copies, waits for them, and re-layouts: 0.03 us -> 2.67 us
    pallas_call x1, Pallas kernels: 7.28 us -> 6.52 us  [pair_bias(): pl.pallas_call(bias_kernel, in_specs=[pl.BlockSpec(memory_space=pltpu.HBM...]
where the time goes in v2:
time: 70.7 us; the launch traced here: 70.4 us
  starting transfers between devices  32.3 us (46%)
  waiting for transfers between devices  19.4 us (27%)
  Pallas kernels  15.8 us (22%)
  local copies, waits for them, and re-layouts  2.67 us (4%)
    ppermute x17, starting transfers between devices, send(): return lax.ppermute(value, AXES, moves(target))  32.3 us
    ppermute x17, waiting for transfers between devices, send(): return lax.ppermute(value, AXES, moves(target))  19.4 us
    pallas_call x1, Pallas kernels, pair_bias(): pl.pallas_call(bias_kernel, in_specs=[pl.BlockSpec(memory_space=pltpu.HBM...  6.52 us
    pallas_call x4, Pallas kernels, attend(): pl.pallas_call(functools.partial(attend_kernel, v), in_specs=[whole()] *...  4.94 us
    unnamed x20, local copies, waits for them, and re-layouts  2.67 us
    pallas_call x1, Pallas kernels, fetch(): pl.pallas_call(fetch_kernel, in_specs=[pl.BlockSpec(memory_space=pltpu.HB...  2.46 us
  transfers between devices with their start and end apart: 17, of which 5 were waited for; matrix products, arithmetic and copies ran while one was open for 0% of the time, Pallas kernels for 12%

profile of v2, /device:TPU:16, one launch (start us, length us, event | category | flops | bytes accessed | tf_op | source)
XLA Modules:
  0.0 70.4 jit_solution(6454816029125750574)
XLA Ops:
  0.0 0.7 copy-done.5
  0.7 0.7 copy-done.6
  1.3 0.7 copy-done.7
  2.0 0.7 copy-done.8
  2.7 6.5 %pair_bias.1.bias_a = f32[4,128,128]{2,1,0:T(8,128)S(1)} custom-call(bf16[128,128,128]{2,1,0:T(8,128)(2,1)} %pair_rep.3, f32[1,128]{1,0:T(1,128)S(1)} %bitcast.10, f32[1,128]{1,0:T(1,128)S(1)} %bitcast.12, bf16[4,128]{1,0:T(4,128)(2,1)S(1)} %bitcast.13, s32[1,128]{1,0:T(1,128)S(1)} %bitcast.14), custom_call_target="tpu_custom_call" | custom-call | flops 8388608 | bytes 4194304 | tf_op jit(solution)/shard_map/pair_bias/pallas_call | solution.py:135
  9.2 2.0 %collective-permute-start.8 = (f32[4,128,128]{2,1,0:T(8,128)S(1)}, f32[4,128,128]{2,1,0:T(8,128)S(1)}, u32[]{:S(2)}, u32[]{:S(2)}) collective-permute-start(f32[4,128,128]{2,1,0:T(8,128)S(1)} %pair_bias.1.bias_a), channel_id=1, source_target_pairs={{0,2},{1,3},{2,0},{3,1},{4,6},{5,7},{6,4},{7,5},{8,10},{9,11},{10,... | collective-permute-start | bytes 786440 | tf_op jit(solution)/shard_map/ppermute | solution.py:295
  11.2 2.5 %fetch.1 = bf16[2,128,128]{2,1,0:T(8,128)(2,1)} custom-call(s32[2]{0:T(128)} %row_ids.1, bf16[128,128,128]{2,1,0:T(8,128)(2,1)} %pair_rep.3, f32[1,128]{1,0:T(1,128)} %bitcast.9, f32[1,128]{1,0:T(1,128)} %bitcast.11), custom_call_target="tpu_custom_call" | custom-call | flops 327680 | bytes 131072 | tf_op jit(solution)/shard_map/fetch/pallas_call | solution.py:62
  13.7 1.5 %collective-permute-start = (bf16[2,128,128]{2,1,0:T(8,128)(2,1)}, bf16[2,128,128]{2,1,0:T(8,128)(2,1)S(1)}, u32[]{:S(2)}, u32[]{:S(2)}) collective-permute-start(bf16[2,128,128]{2,1,0:T(8,128)(2,1)} %fetch.1), channel_id=1, source_target_pairs={{0,0},{1,16},{2,32},{3,48},{4,4},{5,20},{6,36},{7,52},{8,8},{9,24}... | collective-permute-start | bytes 196616 | tf_op jit(solution)/shard_map/ppermute | solution.py:295
  15.2 5.9 %collective-permute-start.4 = (bf16[2,128,128]{2,1,0:T(8,128)(2,1)}, bf16[2,128,128]{2,1,0:T(8,128)(2,1)S(1)}, u32[]{:S(2)}, u32[]{:S(2)}) collective-permute-start(bf16[2,128,128]{2,1,0:T(8,128)(2,1)} %fetch.1), channel_id=1, source_target_pairs={{0,48},{1,0},{2,16},{3,32},{4,52},{5,4},{6,20},{7,36},{8,56},{9,8}... | collective-permute-start | bytes 196616 | tf_op jit(solution)/shard_map/ppermute | solution.py:295
  21.1 3.4 %collective-permute-start.3 = (bf16[2,128,128]{2,1,0:T(8,128)(2,1)}, bf16[2,128,128]{2,1,0:T(8,128)(2,1)S(1)}, u32[]{:S(2)}, u32[]{:S(2)}) collective-permute-start(bf16[2,128,128]{2,1,0:T(8,128)(2,1)} %fetch.1), channel_id=1, source_target_pairs={{0,32},{1,48},{2,0},{3,16},{4,36},{5,52},{6,4},{7,20},{8,40},{9,56... | collective-permute-start | bytes 196616 | tf_op jit(solution)/shard_map/ppermute | solution.py:295
  24.5 2.8 %collective-permute-start.2 = (bf16[2,128,128]{2,1,0:T(8,128)(2,1)}, bf16[2,128,128]{2,1,0:T(8,128)(2,1)S(1)}, u32[]{:S(2)}, u32[]{:S(2)}) collective-permute-start(bf16[2,128,128]{2,1,0:T(8,128)(2,1)} %fetch.1), channel_id=1, source_target_pairs={{0,16},{1,32},{2,48},{3,0},{4,20},{5,36},{6,52},{7,4},{8,24},{9,40... | collective-permute-start | bytes 196616 | tf_op jit(solution)/shard_map/ppermute | solution.py:295
  27.3 2.0 %collective-permute-done.3 = bf16[2,128,128]{2,1,0:T(8,128)(2,1)S(1)} collective-permute-done((bf16[2,128,128]{2,1,0:T(8,128)(2,1)}, bf16[2,128,128]{2,1,0:T(8,128)(2,1)S(1)}, u32[]{:S(2)}, u32[]{:S(2)}) %collective-permute-start.3) | collective-permute-done | bytes 65568 | tf_op jit(solution)/shard_map/ppermute | solution.py:295
  29.3 0.8 %collective-permute-done.2 = bf16[2,128,128]{2,1,0:T(8,128)(2,1)S(1)} collective-permute-done((bf16[2,128,128]{2,1,0:T(8,128)(2,1)}, bf16[2,128,128]{2,1,0:T(8,128)(2,1)S(1)}, u32[]{:S(2)}, u32[]{:S(2)}) %collective-permute-start.2) | collective-permute-done | bytes 65568 | tf_op jit(solution)/shard_map/ppermute | solution.py:295
  30.1 1.4 %collective-permute-start.5 = (bf16[4,2,128,128]{3,2,1,0:T(8,128)(2,1)S(1)}, bf16[4,2,128,128]{3,2,1,0:T(8,128)(2,1)S(1)}, u32[]{:S(2)}, u32[]{:S(2)}) collective-permute-start(bf16[4,2,128,128]{3,2,1,0:T(8,128)(2,1)S(1)} %pad_maximum_fusion.refs_0_), channel_id=1, source_target_pairs={{0,64},{1,65},{2,66},{3,67},{4,68},{5,69},{6,70},{7,71},{8,72},{9,... | collective-permute-start | bytes 786440 | tf_op jit(solution)/shard_map/ppermute | solution.py:295
  31.4 0.6 collective-permute-start.6
  32.1 1.1 %collective-permute-start.7 = (bf16[4,2,128,128]{3,2,1,0:T(8,128)(2,1)S(1)}, bf16[4,2,128,128]{3,2,1,0:T(8,128)(2,1)S(1)}, u32[]{:S(2)}, u32[]{:S(2)}) collective-permute-start(bf16[4,2,128,128]{3,2,1,0:T(8,128)(2,1)S(1)} %pad_maximum_fusion.refs_0_), channel_id=1, source_target_pairs={{0,192},{1,193},{2,194},{3,195},{4,196},{5,197},{6,198},{7,199},{8... | collective-permute-start | bytes 786440 | tf_op jit(solution)/shard_map/ppermute | solution.py:295
  33.1 0.5 collective-permute-start.10
  33.6 10.5 %collective-permute-done.5.refs_1_ = bf16[4,2,128,128]{3,2,1,0:T(8,128)(2,1)S(1)} collective-permute-done((bf16[4,2,128,128]{3,2,1,0:T(8,128)(2,1)S(1)}, bf16[4,2,128,128]{3,2,1,0:T(8,128)(2,1)S(1)}, u32[]{:S(2)}, u32[]{:S(2)}) %collective-permute-start.5) | collective-permute-done | bytes 262176 | tf_op jit(solution)/shard_map/ppermute | solution.py:295
  44.2 4.3 %collective-permute-start.12 = (bf16[2,128,128]{2,1,0:T(8,128)(2,1)S(1)}, bf16[2,128,128]{2,1,0:T(8,128)(2,1)S(1)}, u32[]{:S(2)}, u32[]{:S(2)}) collective-permute-start(bf16[2,128,128]{2,1,0:T(8,128)(2,1)S(1)} %collective-permute-done), channel_id=1, source_target_pairs={{0,4},{1,5},{2,6},{3,7},{4,68},{5,69},{6,70},{7,71},{8,132},{9,133... | collective-permute-start | bytes 196616 | tf_op jit(solution)/shard_map/ppermute | solution.py:295
  48.4 0.7 collective-permute-start.14
  49.1 0.8 %project.1 = (bf16[4,2,128,512]{3,2,1,0:T(8,128)(2,1)S(1)}, bf16[4,2,512,128]{3,2,1,0:T(8,128)(2,1)S(1)}) custom-call(bf16[4,2,128,128]{3,2,1,0:T(8,128)(2,1)S(1)} %pad_maximum_fusion.refs_0_, bf16[4,2,128,128]{3,2,1,0:T(8,128)(2,1)S(1)} %collective-permute-done.5.refs_1_, bf16[4,2,128,128]{3,2,1,0:T(8,128)(2,1)S(1)} %collective-permute-done.6.refs_2_, ...), custom_call_target="tpu_custom_call" | custom-call | flops 268435456 | bytes 3145728 | tf_op jit(solution)/shard_map/project/pallas_call | solution.py:176
  49.9 1.5 %collective-permute-done.1.rows = bf16[2,128,128]{2,1,0:T(8,128)(2,1)S(1)} collective-permute-done((bf16[2,128,128]{2,1,0:T(8,128)(2,1)S(1)}, bf16[2,128,128]{2,1,0:T(8,128)(2,1)S(1)}, u32[]{:S(2)}, u32[]{:S(2)}) %collective-permute-start.1) | collective-permute-done | bytes 65568 | tf_op jit(solution)/shard_map/ppermute | solution.py:295
  51.5 4.8 %collective-permute-start.16 = (bf16[2,128,128]{2,1,0:T(8,128)(2,1)S(1)}, bf16[2,128,128]{2,1,0:T(8,128)(2,1)S(1)}, u32[]{:S(2)}, u32[]{:S(2)}) collective-permute-start(bf16[2,128,128]{2,1,0:T(8,128)(2,1)S(1)} %collective-permute-done), channel_id=1, source_target_pairs={{0,0},{1,1},{2,2},{3,3},{4,64},{5,65},{6,66},{7,67},{8,128},{9,129... | collective-permute-start | bytes 196616 | tf_op jit(solution)/shard_map/ppermute | solution.py:295
  56.3 1.2 %shard_map.118 = bf16[2,144,128]{2,1,0:T(8,128)(2,1)S(1)} custom-call(bf16[2,128,128]{2,1,0:T(8,128)(2,1)S(1)} %collective-permute-done.1.rows, bf16[4,2,128,512]{3,2,1,0:T(8,128)(2,1)S(1)} %get-tuple-element.9.keys, bf16[4,2,512,128]{3,2,1,0:T(8,128)(2,1)S(1)} %get-tuple-element.10.values, f32[4,128,128]{2,1,0:T(8,128)S(1)} %pair_bias.1.bias_a, ...), custom_call_target="tpu_custom_call" | custom-call | flops 268435456 | bytes 2097152 | tf_op jit(solution)/shard_map/pallas_call | solution.py:232
  57.5 0.1 collective-permute-start.11
  57.6 1.2 %shard_map.119 = bf16[2,144,128]{2,1,0:T(8,128)(2,1)S(1)} custom-call(bf16[2,128,128]{2,1,0:T(8,128)(2,1)S(1)} %collective-permute-done.12.rows, bf16[4,2,128,512]{3,2,1,0:T(8,128)(2,1)S(1)} %get-tuple-element.9.keys, bf16[4,2,512,128]{3,2,1,0:T(8,128)(2,1)S(1)} %get-tuple-element.10.values, f32[4,128,128]{2,1,0:T(8,128)S(1)} %pair_bias.1.bias_a, ...), custom_call_target="tpu_custom_call" | custom-call | flops 268435456 | bytes 2097152 | tf_op jit(solution)/shard_map/pallas_call | solution.py:232
  58.8 3.3 %collective-permute-start.13 = (bf16[2,144,128]{2,1,0:T(8,128)(2,1)S(1)}, bf16[2,144,128]{2,1,0:T(8,128)(2,1)S(1)}, u32[]{:S(2)}, u32[]{:S(2)}) collective-permute-start(bf16[2,144,128]{2,1,0:T(8,128)(2,1)S(1)} %shard_map.119), channel_id=1, source_target_pairs={{0,12},{1,13},{2,14},{3,15},{4,0},{5,1},{6,2},{7,3},{8,4},{9,5},{1... | collective-permute-start | bytes 221192 | tf_op jit(solution)/shard_map/ppermute | solution.py:295
  62.1 1.2 %shard_map.120 = bf16[2,144,128]{2,1,0:T(8,128)(2,1)S(1)} custom-call(bf16[2,128,128]{2,1,0:T(8,128)(2,1)S(1)} %collective-permute-done.14.rows, bf16[4,2,128,512]{3,2,1,0:T(8,128)(2,1)S(1)} %get-tuple-element.9.keys, bf16[4,2,512,128]{3,2,1,0:T(8,128)(2,1)S(1)} %get-tuple-element.10.values, f32[4,128,128]{2,1,0:T(8,128)S(1)} %pair_bias.1.bias_a, ...), custom_call_target="tpu_custom_call" | custom-call | flops 268435456 | bytes 2097152 | tf_op jit(solution)/shard_map/pallas_call | solution.py:232
  63.3 0.1 collective-permute-start.15
  63.4 1.3 %shard_map.121 = (bf16[2,128,128]{2,1,0:T(8,128)(2,1)S(1)}, bf16[2,144,128]{2,1,0:T(8,128)(2,1)S(1)}) custom-call(bf16[2,128,128]{2,1,0:T(8,128)(2,1)S(1)} %collective-permute-done.16.rows, bf16[4,2,128,512]{3,2,1,0:T(8,128)(2,1)S(1)} %get-tuple-element.9.keys, bf16[4,2,512,128]{3,2,1,0:T(8,128)(2,1)S(1)} %get-tuple-element.10.values, ...), custom_call_target="tpu_custom_call" | custom-call | flops 268435456 | bytes 2097152 | tf_op jit(solution)/shard_map/pallas_call | solution.py:232
  64.7 4.5 %collective-permute-done.15.third = bf16[2,144,128]{2,1,0:T(8,128)(2,1)S(1)} collective-permute-done((bf16[2,144,128]{2,1,0:T(8,128)(2,1)S(1)}, bf16[2,144,128]{2,1,0:T(8,128)(2,1)S(1)}, u32[]{:S(2)}, u32[]{:S(2)}) %collective-permute-start.15) | collective-permute-done | bytes 73760 | tf_op jit(solution)/shard_map/ppermute | solution.py:295
  69.2 1.1 %finish.1 = bf16[2,128,128]{2,1,0:T(8,128)(2,1)} custom-call(bf16[2,144,128]{2,1,0:T(8,128)(2,1)S(1)} %collective-permute-done.11.first, bf16[2,144,128]{2,1,0:T(8,128)(2,1)S(1)} %collective-permute-done.13.second, bf16[2,144,128]{2,1,0:T(8,128)(2,1)S(1)} %collective-permute-done.15.third, bf16[2,144,128]{2,1,0:T(8,128)(2,1)S(1)} %get-tuple-element.11.fourth, ...), custom_call_target="tpu_custom_call" | custom-call | flops 16777216 | bytes 524288 | tf_op jit(solution)/shard_map/finish/pallas_call | solution.py:274
  (31 shorter events, 0.1 us)
Async XLA Ops:
  0.0 0.7 copy-start.5
  0.7 0.7 copy-start.6
  1.3 0.7 copy-start.7
  2.0 0.7 copy-start.8
  2.6 46.5 %copy-start.3 = (bf16[128,128]{1,0:T(8,128)(2,1)S(1)}, bf16[128,128]{1,0:T(8,128)(2,1)}, u32[]{:S(2)}) copy-start(bf16[128,128]{1,0:T(8,128)(2,1)} %refs_4_.1) | copy-start | bytes 98308
  2.6 46.5 %copy-start.4 = (bf16[128,128]{1,0:T(8,128)(2,1)S(1)}, bf16[128,128]{1,0:T(8,128)(2,1)}, u32[]{:S(2)}) copy-start(bf16[128,128]{1,0:T(8,128)(2,1)} %refs_5_.1) | copy-start | bytes 98308
  2.7 53.6 %copy-start = (bf16[128,128]{1,0:T(8,128)(2,1)S(1)}, bf16[128,128]{1,0:T(8,128)(2,1)}, u32[]{:S(2)}) copy-start(bf16[128,128]{1,0:T(8,128)(2,1)} %w_query.7) | copy-start | bytes 98308
  9.2 23.9 %collective-permute-start.8 = (f32[4,128,128]{2,1,0:T(8,128)S(1)}, f32[4,128,128]{2,1,0:T(8,128)S(1)}, u32[]{:S(2)}, u32[]{:S(2)}) collective-permute-start(f32[4,128,128]{2,1,0:T(8,128)S(1)} %pair_bias.1.bias_a), channel_id=1, source_target_pairs={{0,2},{1,3},{2,0},{3,1},{4,6},{5,7},{6,4},{7,5},{8,10},{9,11},{10,... | collective-permute-start | bytes 786440 | tf_op jit(solution)/shard_map/ppermute | solution.py:295
  13.7 13.6 %collective-permute-start = (bf16[2,128,128]{2,1,0:T(8,128)(2,1)}, bf16[2,128,128]{2,1,0:T(8,128)(2,1)S(1)}, u32[]{:S(2)}, u32[]{:S(2)}) collective-permute-start(bf16[2,128,128]{2,1,0:T(8,128)(2,1)} %fetch.1), channel_id=1, source_target_pairs={{0,0},{1,16},{2,32},{3,48},{4,4},{5,20},{6,36},{7,52},{8,8},{9,24}... | collective-permute-start | bytes 196616 | tf_op jit(solution)/shard_map/ppermute | solution.py:295
  15.2 12.1 %collective-permute-start.4 = (bf16[2,128,128]{2,1,0:T(8,128)(2,1)}, bf16[2,128,128]{2,1,0:T(8,128)(2,1)S(1)}, u32[]{:S(2)}, u32[]{:S(2)}) collective-permute-start(bf16[2,128,128]{2,1,0:T(8,128)(2,1)} %fetch.1), channel_id=1, source_target_pairs={{0,48},{1,0},{2,16},{3,32},{4,52},{5,4},{6,20},{7,36},{8,56},{9,8}... | collective-permute-start | bytes 196616 | tf_op jit(solution)/shard_map/ppermute | solution.py:295
  21.1 8.2 %collective-permute-start.3 = (bf16[2,128,128]{2,1,0:T(8,128)(2,1)}, bf16[2,128,128]{2,1,0:T(8,128)(2,1)S(1)}, u32[]{:S(2)}, u32[]{:S(2)}) collective-permute-start(bf16[2,128,128]{2,1,0:T(8,128)(2,1)} %fetch.1), channel_id=1, source_target_pairs={{0,32},{1,48},{2,0},{3,16},{4,36},{5,52},{6,4},{7,20},{8,40},{9,56... | collective-permute-start | bytes 196616 | tf_op jit(solution)/shard_map/ppermute | solution.py:295
  24.5 5.5 %collective-permute-start.2 = (bf16[2,128,128]{2,1,0:T(8,128)(2,1)}, bf16[2,128,128]{2,1,0:T(8,128)(2,1)S(1)}, u32[]{:S(2)}, u32[]{:S(2)}) collective-permute-start(bf16[2,128,128]{2,1,0:T(8,128)(2,1)} %fetch.1), channel_id=1, source_target_pairs={{0,16},{1,32},{2,48},{3,0},{4,20},{5,36},{6,52},{7,4},{8,24},{9,40... | collective-permute-start | bytes 196616 | tf_op jit(solution)/shard_map/ppermute | solution.py:295
  30.1 14.1 %collective-permute-start.5 = (bf16[4,2,128,128]{3,2,1,0:T(8,128)(2,1)S(1)}, bf16[4,2,128,128]{3,2,1,0:T(8,128)(2,1)S(1)}, u32[]{:S(2)}, u32[]{:S(2)}) collective-permute-start(bf16[4,2,128,128]{3,2,1,0:T(8,128)(2,1)S(1)} %pad_maximum_fusion.refs_0_), channel_id=1, source_target_pairs={{0,64},{1,65},{2,66},{3,67},{4,68},{5,69},{6,70},{7,71},{8,72},{9,... | collective-permute-start | bytes 786440 | tf_op jit(solution)/shard_map/ppermute | solution.py:295
  31.4 12.7 %collective-permute-start.6 = (bf16[4,2,128,128]{3,2,1,0:T(8,128)(2,1)S(1)}, bf16[4,2,128,128]{3,2,1,0:T(8,128)(2,1)S(1)}, u32[]{:S(2)}, u32[]{:S(2)}) collective-permute-start(bf16[4,2,128,128]{3,2,1,0:T(8,128)(2,1)S(1)} %pad_maximum_fusion.refs_0_), channel_id=1, source_target_pairs={{0,128},{1,129},{2,130},{3,131},{4,132},{5,133},{6,134},{7,135},{8... | collective-permute-start | bytes 786440 | tf_op jit(solution)/shard_map/ppermute | solution.py:295
  32.1 16.4 %collective-permute-start.7 = (bf16[4,2,128,128]{3,2,1,0:T(8,128)(2,1)S(1)}, bf16[4,2,128,128]{3,2,1,0:T(8,128)(2,1)S(1)}, u32[]{:S(2)}, u32[]{:S(2)}) collective-permute-start(bf16[4,2,128,128]{3,2,1,0:T(8,128)(2,1)S(1)} %pad_maximum_fusion.refs_0_), channel_id=1, source_target_pairs={{0,192},{1,193},{2,194},{3,195},{4,196},{5,197},{6,198},{7,199},{8... | collective-permute-start | bytes 786440 | tf_op jit(solution)/shard_map/ppermute | solution.py:295
  33.1 23.1 %collective-permute-start.9 = (f32[4,128,128]{2,1,0:T(8,128)S(1)}, f32[4,128,128]{2,1,0:T(8,128)S(1)}, u32[]{:S(2)}, u32[]{:S(2)}) collective-permute-start(f32[4,128,128]{2,1,0:T(8,128)S(1)} %pair_bias.1.bias_a), channel_id=1, source_target_pairs={{0,1},{1,0},{2,3},{3,2},{4,5},{5,4},{6,7},{7,6},{8,9},{9,8},{10,11... | collective-permute-start | bytes 786440 | tf_op jit(solution)/shard_map/ppermute | solution.py:295
  33.1 23.1 %collective-permute-start.10 = (f32[4,128,128]{2,1,0:T(8,128)S(1)}, f32[4,128,128]{2,1,0:T(8,128)S(1)}, u32[]{:S(2)}, u32[]{:S(2)}) collective-permute-start(f32[4,128,128]{2,1,0:T(8,128)S(1)} %collective-permute-done.8.bias_b), channel_id=1, source_target_pairs={{0,1},{1,0},{2,3},{3,2},{4,5},{5,4},{6,7},{7,6},{8,9},{9,8},{10,11... | collective-permute-start | bytes 786440 | tf_op jit(solution)/shard_map/ppermute | solution.py:295
  44.2 7.3 %collective-permute-start.1 = (bf16[2,128,128]{2,1,0:T(8,128)(2,1)S(1)}, bf16[2,128,128]{2,1,0:T(8,128)(2,1)S(1)}, u32[]{:S(2)}, u32[]{:S(2)}) collective-permute-start(bf16[2,128,128]{2,1,0:T(8,128)(2,1)S(1)} %collective-permute-done), channel_id=1, source_target_pairs={{0,12},{1,13},{2,14},{3,15},{4,76},{5,77},{6,78},{7,79},{8,140},{9... | collective-permute-start | bytes 196616 | tf_op jit(solution)/shard_map/ppermute | solution.py:295
  44.2 13.4 %collective-permute-start.12 = (bf16[2,128,128]{2,1,0:T(8,128)(2,1)S(1)}, bf16[2,128,128]{2,1,0:T(8,128)(2,1)S(1)}, u32[]{:S(2)}, u32[]{:S(2)}) collective-permute-start(bf16[2,128,128]{2,1,0:T(8,128)(2,1)S(1)} %collective-permute-done), channel_id=1, source_target_pairs={{0,4},{1,5},{2,6},{3,7},{4,68},{5,69},{6,70},{7,71},{8,132},{9,133... | collective-permute-start | bytes 196616 | tf_op jit(solution)/shard_map/ppermute | solution.py:295
  48.4 13.7 %collective-permute-start.14 = (bf16[2,128,128]{2,1,0:T(8,128)(2,1)S(1)}, bf16[2,128,128]{2,1,0:T(8,128)(2,1)S(1)}, u32[]{:S(2)}, u32[]{:S(2)}) collective-permute-start(bf16[2,128,128]{2,1,0:T(8,128)(2,1)S(1)} %collective-permute-done), channel_id=1, source_target_pairs={{0,8},{1,9},{2,10},{3,11},{4,72},{5,73},{6,74},{7,75},{8,136},{9,1... | collective-permute-start | bytes 196616 | tf_op jit(solution)/shard_map/ppermute | solution.py:295
  51.5 11.9 %collective-permute-start.16 = (bf16[2,128,128]{2,1,0:T(8,128)(2,1)S(1)}, bf16[2,128,128]{2,1,0:T(8,128)(2,1)S(1)}, u32[]{:S(2)}, u32[]{:S(2)}) collective-permute-start(bf16[2,128,128]{2,1,0:T(8,128)(2,1)S(1)} %collective-permute-done), channel_id=1, source_target_pairs={{0,0},{1,1},{2,2},{3,3},{4,64},{5,65},{6,66},{7,67},{8,128},{9,129... | collective-permute-start | bytes 196616 | tf_op jit(solution)/shard_map/ppermute | solution.py:295
  56.3 7.1 %copy-start.1 = (bf16[128,128]{1,0:T(8,128)(2,1)S(1)}, bf16[128,128]{1,0:T(8,128)(2,1)}, u32[]{:S(2)}) copy-start(bf16[128,128]{1,0:T(8,128)(2,1)} %rest_0_.1) | copy-start | bytes 98308
  56.3 7.1 %copy-start.9 = (f32[128]{0:T(128)S(1)}, f32[128]{0:T(128)}, u32[]{:S(2)}) copy-start(f32[128]{0:T(128)} %param.21) | copy-start | bytes 1540
  57.5 11.7 %copy-start.2 = (bf16[128,128]{1,0:T(8,128)(2,1)S(1)}, bf16[128,128]{1,0:T(8,128)(2,1)}, u32[]{:S(2)}) copy-start(bf16[128,128]{1,0:T(8,128)(2,1)} %w_out.1) | copy-start | bytes 98308
  57.5 7.2 %collective-permute-start.11 = (bf16[2,144,128]{2,1,0:T(8,128)(2,1)S(1)}, bf16[2,144,128]{2,1,0:T(8,128)(2,1)S(1)}, u32[]{:S(2)}, u32[]{:S(2)}) collective-permute-start(bf16[2,144,128]{2,1,0:T(8,128)(2,1)S(1)} %shard_map.118), channel_id=1, source_target_pairs={{0,4},{1,5},{2,6},{3,7},{4,8},{5,9},{6,10},{7,11},{8,12},{9,13},{1... | collective-permute-start | bytes 221192 | tf_op jit(solution)/shard_map/ppermute | solution.py:295
  58.8 5.9 %collective-permute-start.13 = (bf16[2,144,128]{2,1,0:T(8,128)(2,1)S(1)}, bf16[2,144,128]{2,1,0:T(8,128)(2,1)S(1)}, u32[]{:S(2)}, u32[]{:S(2)}) collective-permute-start(bf16[2,144,128]{2,1,0:T(8,128)(2,1)S(1)} %shard_map.119), channel_id=1, source_target_pairs={{0,12},{1,13},{2,14},{3,15},{4,0},{5,1},{6,2},{7,3},{8,4},{9,5},{1... | collective-permute-start | bytes 221192 | tf_op jit(solution)/shard_map/ppermute | solution.py:295
  63.3 5.9 %collective-permute-start.15 = (bf16[2,144,128]{2,1,0:T(8,128)(2,1)S(1)}, bf16[2,144,128]{2,1,0:T(8,128)(2,1)S(1)}, u32[]{:S(2)}, u32[]{:S(2)}) collective-permute-start(bf16[2,144,128]{2,1,0:T(8,128)(2,1)S(1)} %shard_map.120), channel_id=1, source_target_pairs={{0,8},{1,9},{2,10},{3,11},{4,12},{5,13},{6,14},{7,15},{8,0},{9,1},... | collective-permute-start | bytes 221192 | tf_op jit(solution)/shard_map/ppermute | solution.py:295
